TPU v7x, 32 devices: a whole 2x2x4 slice. The times are simulated.
32 devices in a mesh: row: 4 (over y, x), col: 8 (over z, core).
Axes of the slice: x: 2, y: 2, z: 4, core: 2. Of those that a mesh axis runs over, the one named last changes fastest.
Arguments:
- user_feats: bfloat16 [4096, 128], P(('row', 'col')), may hold values from -6 to 6
- item_feats: bfloat16 [16384, 128], P(('col', 'row')), may hold values from -6 to 6
- tile_values: bfloat16 [4, 8, 1, 512, 512], P('row', 'col'), may hold values from -0.15625 to 0.15625
- tile_coords: int32 [4, 8, 2, 1], P('row', 'col'), may hold values from 0 to 3, as said below
- tile_count: int32 [4, 8], P('row', 'col'), may hold values from 1 to 1, as said below
Outputs:
- users_next: bfloat16 [4096, 128], P(('row', 'col'))
- items_next: bfloat16 [16384, 128], P(('col', 'row'))
Inputs may be any that keep to these rules, and one draw needn't show every extreme that they name: `tile_coords`: within one device's first tile_count slots the pairs (user tile, item tile) are distinct; the first entry is a user tile below 2, the second an item tile below 4; slots at or after the count carry no tile. `tile_count`: at least one device has all 1 slots live.
All inputs are finite; a program needn't handle non-finite values.
Results may differ from a plain program's by a relative error of at most 0.001.
Values may be sent and summed in bfloat16 or wider, within the bound.
A program may use at most 64 MiB of HBM per device.

v0:
```python
import functools

import jax
import jax.numpy as jnp
from jax import lax
from jax.experimental import pallas as pl
from jax.experimental.pallas import tpu as pltpu
from jax.sharding import PartitionSpec as P

MESH = pl.DeviceIdType.MESH


def gathered(user_feats, item_feats, tile_values, tile_coords, tile_count):
    user_block = lax.all_gather(user_feats, "col", axis=0, tiled=True)
    item_block = lax.all_gather(item_feats, "row", axis=0, tiled=True)
    tiles = tile_values[0, 0]
    coords = tile_coords[0, 0]
    count = tile_count[0, 0]
    slots = tiles.shape[0]
    size = tiles.shape[1]
    width = user_block.shape[1]
    user_tiles = user_block.shape[0] // size
    item_tiles = item_block.shape[0] // size
    live = jnp.arange(slots) < count
    pick_user = ((coords[0][:, None] == jnp.arange(user_tiles)[None, :]) & live[:, None]).astype(
        jnp.bfloat16
    )
    pick_item = (coords[1][:, None] == jnp.arange(item_tiles)[None, :]).astype(jnp.bfloat16)
    user_sel = jnp.einsum(
        "su,uiw->siw",
        pick_user,
        user_block.reshape(user_tiles, size, width),
        preferred_element_type=jnp.float32,
    ).astype(jnp.bfloat16)
    item_sel = jnp.einsum(
        "st,tjw->sjw",
        pick_item,
        item_block.reshape(item_tiles, size, width),
        preferred_element_type=jnp.float32,
    ).astype(jnp.bfloat16)
    to_users = jnp.einsum("sij,sjw->siw", tiles, item_sel, preferred_element_type=jnp.float32)
    to_items = jnp.einsum("sij,siw->sjw", tiles, user_sel, preferred_element_type=jnp.float32)
    part_users = jnp.einsum(
        "su,siw->uiw", pick_user.astype(jnp.float32), to_users, precision=lax.Precision.HIGHEST
    ).reshape(user_tiles * size, width)
    part_items = jnp.einsum(
        "st,sjw->tjw", pick_item.astype(jnp.float32), to_items, precision=lax.Precision.HIGHEST
    ).reshape(item_tiles * size, width)
    users_next = lax.psum_scatter(part_users, "col", scatter_dimension=0, tiled=True)
    items_next = lax.psum_scatter(part_items, "row", scatter_dimension=0, tiled=True)
    return (users_next.astype(jnp.bfloat16), items_next.astype(jnp.bfloat16))


def kernel(
    n_z,
    coords_in,
    count_in,
    user_in,
    item_in,
    tile_in,
    out_u,
    out_i,
    u_all,
    i_all,
    tile_v,
    tile_t,
    meta,
    metas,
    part_u,
    from_p,
    send_z,
    from_z,
    part_i,
    from_1,
    send_2,
    from_2,
    coords,
    count,
    load_sem,
    meta_s,
    meta_r,
    uz_s,
    uz_r,
    up_s,
    up_r,
    ig_s,
    ig_r,
    rp_s,
    rp_r,
    rz_s,
    rz_r,
    r1_s,
    r1_r,
    r2_s,
    r2_r,
):
    row, col = lax.axis_index("row"), lax.axis_index("col")
    y, x = row // 2, row % 2
    z, core = col // 2, col % 2
    row_x, row_y = 2 * y + 1 - x, 2 * (1 - y) + x
    x_dev, y_dev = (row_x, col), (row_y, col)
    p_dev = (row, 2 * z + 1 - core)

    def far_first(at):
        flip = z // (n_z // 2)
        mirrored = z + flip * (n_z - 1 - 2 * z)
        to = n_z - 1 - at
        to = jnp.where(to <= mirrored, to - 1, to)
        return to + flip * (n_z - 1 - 2 * to)

    others = [far_first(at) for at in range(n_z - 1)]
    z_devs = [(row, 2 * at + core) for at in others]
    near_first = others[::-1]
    rows_u, rows_i = user_in.shape[0], item_in.shape[0]
    size = tile_v.shape[-1]
    chunk = rows_i // 4
    pieces = size // rows_u // 2

    def user_slot(at):
        blocks = size // rows_u
        inner = pl.multiple_of(at % blocks * rows_u, rows_u)
        return u_all.at[at // blocks, pl.ds(inner, rows_u)]

    def item_slot(at, part, parts=2):
        rows = rows_i // parts
        return i_all.at[at, pl.ds(part * rows, rows)]

    def copy(src, dst, send, recv, device):
        return pltpu.make_async_remote_copy(
            src_ref=src,
            dst_ref=dst,
            send_sem=send,
            recv_sem=recv,
            device_id=device,
            device_id_type=MESH,
        )

    def arrived(like, recv):
        copy(like, like, recv, recv, x_dev).wait_recv()

    def left(like, send):
        copy(like, like, send, send, x_dev).wait_send()

    barrier = pltpu.get_barrier_semaphore()
    peers = [x_dev, y_dev, p_dev] + z_devs
    for peer in peers:
        pl.semaphore_signal(barrier, inc=1, device_id=peer, device_id_type=MESH)
    loads = [
        pltpu.make_async_copy(user_in, user_slot(col), load_sem.at[0]),
        pltpu.make_async_copy(item_in, i_all.at[row], load_sem.at[1]),
        pltpu.make_async_copy(tile_in, tile_v, load_sem.at[2]),
        pltpu.make_async_copy(coords_in, coords, load_sem.at[3]),
        pltpu.make_async_copy(count_in, count, load_sem.at[4]),
    ]
    for load in loads:
        load.start()

    loads[3].wait()
    loads[4].wait()
    tu, ti = coords[0], coords[1]
    meta[0] = jnp.full(meta.shape[1:], tu, jnp.int32)
    meta[1] = jnp.full(meta.shape[1:], ti, jnp.int32)
    meta[2] = jnp.full(meta.shape[1:], count[0, 0], jnp.int32)
    my_tu, my_ti, live = meta[0][0:1, :], meta[1][0:1, :], meta[2][0:1, :] > 0
    pl.semaphore_wait(barrier, len(peers))

    def relay_item(at, part, recv, device):
        piece = item_slot(at, part, 4)
        copy(piece, piece, ig_s.at[0], ig_r.at[recv], device).start()

    loads[0].wait()
    own = user_slot(col)
    for device in z_devs:
        copy(own, own, uz_s.at[0], uz_r.at[z], device).start()
    copy(own, own, up_s.at[0], up_r.at[0], p_dev).start()
    loads[1].wait()
    for part in range(2):
        relay_item(row, part, part, x_dev)
        relay_item(row, 2 + part, 2 + part, y_dev)
    for part, device in ((1, x_dev), (0, y_dev)):
        piece = item_slot(row, part)
        copy(piece, piece, ig_s.at[0], ig_r.at[4], device).start()
    for at, device in enumerate((x_dev, y_dev, p_dev)):
        copy(meta, metas.at[at], meta_s.at[0], meta_r.at[0], device).start()
    meta_x, meta_y, meta_p = metas.at[0], metas.at[1], metas.at[2]

    loads[2].wait()
    tile_t[...] = tile_v[...].reshape(size, size).T

    for part in range(2):
        arrived(item_slot(row_x, part, 4), ig_r.at[part])
        relay_item(row_x, part, 4, y_dev)
        arrived(item_slot(row_y, 2 + part, 4), ig_r.at[2 + part])
        relay_item(row_y, 2 + part, 4, x_dev)
    for at in near_first:
        slot = user_slot(2 * at + core)
        arrived(slot, uz_r.at[at])
        copy(slot, slot, up_s.at[0], up_r.at[0], p_dev).start()
    half_users = u_all.at[pl.ds(0, u_all.shape[0] // 2)]
    arrived(half_users, up_r.at[0])

    user_sel = u_all[tu]
    user_sel = jnp.where(live, user_sel, 0.0).astype(user_sel.dtype)
    part_i[...] = jnp.dot(
        tile_t[...], user_sel, preferred_element_type=jnp.float32
    ).reshape(part_i.shape)
    for c in (0, 2, 1, 3):
        copy(
            part_i.at[c], from_1.at[c], r1_s.at[0], r1_r.at[c], x_dev if c < 2 else y_dev
        ).start()

    arrived(i_all.at[pl.ds(0, 2)], ig_r.at[4])
    item_sel = i_all[ti]
    item_sel = jnp.where(live, item_sel, 0.0).astype(item_sel.dtype)

    def multiply(owner):
        rows = jnp.concatenate([tile_v[2 * h + owner] for h in range(pieces)], axis=0)
        product = jnp.dot(rows, item_sel, preferred_element_type=jnp.float32)
        for h in range(pieces):
            part_u[2 * h + owner] = product[h * rows_u : (h + 1) * rows_u]

    multiply(1 - core)
    for h in range(pieces):
        copy(part_u.at[2 * h + 1 - core], from_p.at[h], rp_s.at[0], rp_r.at[0], p_dev).start()
    multiply(core)
    arrived(metas, meta_r.at[0])

    def second(c):
        other, owner, device = (
            (meta_x, row_y, y_dev) if c < 2 else (meta_y, row_x, x_dev)
        )
        theirs = other[1][0:1, :]
        arrived(from_1.at[c], r1_r.at[c])
        send_2[c] = jnp.where(my_ti == owner, part_i[c], 0.0) + jnp.where(
            theirs == owner, from_1[c], 0.0
        )
        copy(send_2.at[c], from_2.at[c], r2_s.at[0], r2_r.at[c], device).start()

    partner_tu = meta_p[0][0:1, :]
    arrived(from_p, rp_r.at[0])
    for at, device in list(zip(others, z_devs)) + [(z, None)]:
        tile, h = at // pieces, at % pieces
        send_z[at] = jnp.where(my_tu == tile, part_u[2 * h + core], 0.0) + jnp.where(
            partner_tu == tile, from_p[h], 0.0
        )
        if device is not None:
            copy(send_z.at[at], from_z.at[z], rz_s.at[0], rz_r.at[0], device).start()

    for c in (0, 2, 1, 3):
        second(c)

    for c in (0, 2, 1, 3):
        theirs = (meta_x if c < 2 else meta_y)[1][0:1, :]
        mine = jnp.where(my_ti == row, part_i[c], 0.0) + jnp.where(theirs == row, from_1[c], 0.0)
        arrived(from_2.at[c], r2_r.at[c])
        out_i[pl.ds(c * chunk, chunk), :] = (mine + from_2[c]).astype(out_i.dtype)

    total = send_z[z]
    arrived(from_z.at[pl.ds(0, n_z - 1)], rz_r.at[0])
    for at in near_first:
        total = total + from_z[at]
    out_u[...] = total.astype(out_u.dtype)

    left(u_all.at[0, pl.ds(0, (n_z - 1) * rows_u)], uz_s.at[0])
    left(half_users, up_s.at[0])
    left(i_all.at[pl.ds(0, 3)], ig_s.at[0])
    left(metas, meta_s.at[0])
    left(part_i, r1_s.at[0])
    left(from_p, rp_s.at[0])
    left(send_2, r2_s.at[0])
    left(send_z.at[pl.ds(0, n_z - 1)], rz_s.at[0])


def put(users, items, out_u, out_i, sems):
    copies = [
        pltpu.make_async_copy(users, out_u, sems.at[0]),
        pltpu.make_async_copy(items, out_i, sems.at[1]),
    ]
    for c in copies:
        c.start()
    for c in copies:
        c.wait()


def planned(user_feats, item_feats, tile_values, tile_coords, tile_count, *, n_z):
    rows_u, width = user_feats.shape
    rows_i = item_feats.shape[0]
    size = tile_values.shape[-1]
    f32, bf16, dma = jnp.float32, jnp.bfloat16, pltpu.SemaphoreType.DMA
    blocks = size // rows_u
    vmem = pl.BlockSpec(memory_space=pltpu.VMEM)
    anywhere = pl.BlockSpec(memory_space=pl.ANY)
    quarter = (4, rows_i // 4, width)
    arrivals = [1, n_z, 1, 5, 1, 1, 4, 4]
    outs = pl.pallas_call(
        functools.partial(kernel, n_z),
        out_shape=(pltpu.VMEM((rows_u, width), bf16), pltpu.VMEM((rows_i, width), bf16)),
        in_specs=[anywhere] * 5,
        out_specs=(vmem, vmem),
        scratch_shapes=[
            pltpu.VMEM((2 * n_z * rows_u // size, size, width), bf16),
            pltpu.VMEM((4, rows_i, width), bf16),
            pltpu.VMEM((blocks, rows_u, size), bf16),
            pltpu.VMEM((size, size), bf16),
            pltpu.VMEM((3, 8, width), jnp.int32),
            pltpu.VMEM((3, 3, 8, width), jnp.int32),
            pltpu.VMEM((blocks, rows_u, width), f32),
            pltpu.VMEM((blocks // 2, rows_u, width), f32),
            pltpu.VMEM((n_z, rows_u, width), f32),
            pltpu.VMEM((n_z, rows_u, width), f32),
            pltpu.VMEM(quarter, f32),
            pltpu.VMEM(quarter, f32),
            pltpu.VMEM(quarter, f32),
            pltpu.VMEM(quarter, f32),
            pltpu.SMEM((2,), jnp.int32),
            pltpu.SMEM((1, 1), jnp.int32),
            dma((5,)),
        ]
        + [dma((n,)) for arrival in arrivals for n in (1, arrival)],
        compiler_params=pltpu.CompilerParams(collective_id=0, has_side_effects=True),
    )(
        tile_coords.reshape(2),
        tile_count,
        user_feats,
        item_feats,
        tile_values.reshape(blocks, rows_u, size),
    )
    return pl.pallas_call(
        put,
        out_shape=[jax.ShapeDtypeStruct(out.shape, out.dtype) for out in outs],
        in_specs=[vmem, vmem],
        out_specs=[anywhere, anywhere],
        scratch_shapes=[dma((2,))],
    )(*[pltpu.with_memory_space_constraint(out, pltpu.VMEM) for out in outs])


def solution(mesh):
    n_row, n_col = mesh.shape["row"], mesh.shape["col"]

    def local(user_feats, item_feats, tile_values, tile_coords, tile_count):
        slots, size = tile_values.shape[2], tile_values.shape[3]
        rows_u = user_feats.shape[0]
        fits = (
            n_row == 4
            and n_col % 2 == 0
            and slots == 1
            and item_feats.shape[0] == size
            and size % (2 * rows_u) == 0
            and n_col * rows_u % (2 * size) == 0
            and (n_col // 2 - 1) * rows_u <= size
        )
        args = (user_feats, item_feats, tile_values, tile_coords, tile_count)
        return planned(*args, n_z=n_col // 2) if fits else gathered(*args)

    placed = (
        P(("row", "col"), None),
        P(("col", "row"), None),
        P("row", "col", None, None, None),
        P("row", "col", None, None),
        P("row", "col"),
    )
    return jax.shard_map(
        local,
        mesh=mesh,
        in_specs=placed,
        out_specs=(P(("row", "col"), None), P(("col", "row"), None)),
        check_vma=False,
    )
```

profile of v0, /device:TPU:1, one launch (start us, length us, event | category | flops | bytes accessed | tf_op | source)
XLA Modules:
  0.0 21.9 jit_solution(5649653339247110656)
XLA Ops:
  1.3 19.9 %shard_map.68 = (bf16[128,128]{1,0:T(8,128)(2,1)S(1)}, bf16[512,128]{1,0:T(8,128)(2,1)S(1)}) custom-call(s32[2]{0:T(128)} %bitcast.3, s32[1,1]{1,0:T(1,128)S(6)} %copy.7.count_in, bf16[128,128]{1,0:T(8,128)(2,1)} %user_in.1, bf16[512,128]{1,0:T(8,128)(2,1)} %item_in.1, bf16[4,128,512]{2,1,0:T(8,128)(2,1)} %bitcast.2), custom_call_target="tpu_custom_call" | custom-call | tf_op jit(solution)/shard_map/pallas_call | solution.py:295
  21.2 0.7 %shard_map.69 = (bf16[128,128]{1,0:T(8,128)(2,1)}, bf16[512,128]{1,0:T(8,128)(2,1)}) custom-call(bf16[128,128]{1,0:T(8,128)(2,1)S(1)} %get-tuple-element.4.users, bf16[512,128]{1,0:T(8,128)(2,1)S(1)} %get-tuple-element.5.items), custom_call_target="tpu_custom_call" | custom-call | tf_op jit(solution)/shard_map/pallas_call | solution.py:328
where the time goes:
time: 22 us; the launch traced here: 21.9 us
  Pallas kernels  20.6 us (94%)
  between operations  1.29 us (6%)
    pallas_call x1, Pallas kernels, planned(): pl.pallas_call(functools.partial(kernel, n_z), out_shape=(pltpu.VMEM((row...  19.9 us
    pallas_call x1, Pallas kernels, planned(): pl.pallas_call(put, out_shape=[jax.ShapeDtypeStruct(out.shape, out.dtype)...  0.69 us

commit v1 on v0

--- a/solution.py
+++ b/solution.py
@@ -8,6 +8,8 @@
 from jax.sharding import PartitionSpec as P
 
 MESH = pl.DeviceIdType.MESH
+STEPS = 32760.0
+TINY = 1e-30
 
 
 def gathered(user_feats, item_feats, tile_values, tile_coords, tile_count):
@@ -51,6 +53,26 @@
     return (users_next.astype(jnp.bfloat16), items_next.astype(jnp.bfloat16))
 
 
+def encode(values):
+    rows, width = values.shape
+    groups = values.reshape(rows // 8, 8, width)
+    peak = jnp.maximum(jnp.max(jnp.abs(groups), axis=0), TINY)
+    return encode_by(values, peak), peak
+
+
+def encode_by(values, peak):
+    rows, width = values.shape
+    groups = values.reshape(rows // 8, 8, width)
+    scaled = jnp.round(groups * (STEPS / peak)[None])
+    return scaled.astype(jnp.int32).astype(jnp.int16).reshape(rows, width)
+
+
+def decode(code, peak):
+    rows, width = code.shape
+    groups = code.astype(jnp.int32).astype(jnp.float32).reshape(rows // 8, 8, width)
+    return (groups * (peak * (1.0 / STEPS))[None]).reshape(rows, width)
+
+
 def kernel(
     n_z,
     coords_in,
@@ -69,11 +91,18 @@
     part_u,
     from_p,
     send_z,
+    peak_z,
     from_z,
+    from_zp,
     part_i,
+    send_1,
+    peak_1,
     from_1,
+    from_1p,
     send_2,
+    peak_2,
     from_2,
+    from_2p,
     coords,
     count,
     load_sem,
@@ -89,10 +118,16 @@
     rp_r,
     rz_s,
     rz_r,
+    rzp_s,
+    rzp_r,
     r1_s,
     r1_r,
+    r1p_s,
+    r1p_r,
     r2_s,
     r2_r,
+    r2p_s,
+    r2p_r,
 ):
     row, col = lax.axis_index("row"), lax.axis_index("col")
     y, x = row // 2, row % 2
@@ -201,12 +236,16 @@
 
     user_sel = u_all[tu]
     user_sel = jnp.where(live, user_sel, 0.0).astype(user_sel.dtype)
-    part_i[...] = jnp.dot(
-        tile_t[...], user_sel, preferred_element_type=jnp.float32
-    ).reshape(part_i.shape)
+    product_i = jnp.dot(tile_t[...], user_sel, preferred_element_type=jnp.float32)
+    part_i[...] = product_i.reshape(part_i.shape)
+    code, peak = encode(product_i)
+    peak_1[...] = peak
+    send_1[...] = code.reshape(send_1.shape)
+    for at, device in enumerate((x_dev, y_dev)):
+        copy(peak_1, from_1p.at[at], r1p_s.at[0], r1p_r.at[at], device).start()
     for c in (0, 2, 1, 3):
         copy(
-            part_i.at[c], from_1.at[c], r1_s.at[0], r1_r.at[c], x_dev if c < 2 else y_dev
+            send_1.at[c], from_1.at[c], r1_s.at[0], r1_r.at[c], x_dev if c < 2 else y_dev
         ).start()
 
     arrived(i_all.at[pl.ds(0, 2)], ig_r.at[4])
@@ -231,44 +270,58 @@
         )
         theirs = other[1][0:1, :]
         arrived(from_1.at[c], r1_r.at[c])
-        send_2[c] = jnp.where(my_ti == owner, part_i[c], 0.0) + jnp.where(
-            theirs == owner, from_1[c], 0.0
+        there = decode(from_1[c], from_1p[c // 2])
+        send_2[c], peak_2[c] = encode(
+            jnp.where(my_ti == owner, part_i[c], 0.0) + jnp.where(theirs == owner, there, 0.0)
         )
+        copy(peak_2.at[c], from_2p.at[c], r2p_s.at[0], r2p_r.at[c], device).start()
         copy(send_2.at[c], from_2.at[c], r2_s.at[0], r2_r.at[c], device).start()
 
     partner_tu = meta_p[0][0:1, :]
     arrived(from_p, rp_r.at[0])
     for at, device in list(zip(others, z_devs)) + [(z, None)]:
         tile, h = at // pieces, at % pieces
-        send_z[at] = jnp.where(my_tu == tile, part_u[2 * h + core], 0.0) + jnp.where(
+        both = jnp.where(my_tu == tile, part_u[2 * h + core], 0.0) + jnp.where(
             partner_tu == tile, from_p[h], 0.0
         )
-        if device is not None:
+        if device is None:
+            total = both
+        else:
+            send_z[at], peak_z[at] = encode(both)
+            copy(peak_z.at[at], from_zp.at[z], rzp_s.at[0], rzp_r.at[0], device).start()
             copy(send_z.at[at], from_z.at[z], rz_s.at[0], rz_r.at[0], device).start()
 
+    for at in range(2):
+        arrived(from_1p.at[at], r1p_r.at[at])
     for c in (0, 2, 1, 3):
         second(c)
 
     for c in (0, 2, 1, 3):
         theirs = (meta_x if c < 2 else meta_y)[1][0:1, :]
-        mine = jnp.where(my_ti == row, part_i[c], 0.0) + jnp.where(theirs == row, from_1[c], 0.0)
+        there = decode(from_1[c], from_1p[c // 2])
+        mine = jnp.where(my_ti == row, part_i[c], 0.0) + jnp.where(theirs == row, there, 0.0)
+        arrived(from_2p.at[c], r2p_r.at[c])
         arrived(from_2.at[c], r2_r.at[c])
-        out_i[pl.ds(c * chunk, chunk), :] = (mine + from_2[c]).astype(out_i.dtype)
-
-    total = send_z[z]
+        last = mine + decode(from_2[c], from_2p[c])
+        out_i[pl.ds(c * chunk, chunk), :] = last.astype(out_i.dtype)
+
+    arrived(from_zp.at[pl.ds(0, n_z - 1)], rzp_r.at[0])
     arrived(from_z.at[pl.ds(0, n_z - 1)], rz_r.at[0])
     for at in near_first:
-        total = total + from_z[at]
+        total = total + decode(from_z[at], from_zp[at])
     out_u[...] = total.astype(out_u.dtype)
 
     left(u_all.at[0, pl.ds(0, (n_z - 1) * rows_u)], uz_s.at[0])
     left(half_users, up_s.at[0])
     left(i_all.at[pl.ds(0, 3)], ig_s.at[0])
     left(metas, meta_s.at[0])
-    left(part_i, r1_s.at[0])
+    left(send_1, r1_s.at[0])
+    left(from_1p, r1p_s.at[0])
     left(from_p, rp_s.at[0])
     left(send_2, r2_s.at[0])
+    left(peak_2, r2p_s.at[0])
     left(send_z.at[pl.ds(0, n_z - 1)], rz_s.at[0])
+    left(peak_z.at[pl.ds(0, n_z - 1)], rzp_s.at[0])
 
 
 def put(users, items, out_u, out_i, sems):
@@ -291,7 +344,8 @@
     vmem = pl.BlockSpec(memory_space=pltpu.VMEM)
     anywhere = pl.BlockSpec(memory_space=pl.ANY)
     quarter = (4, rows_i // 4, width)
-    arrivals = [1, n_z, 1, 5, 1, 1, 4, 4]
+    arrivals = [1, n_z, 1, 5, 1, 1, 1, 4, 2, 4, 4]
+    i16 = jnp.int16
     outs = pl.pallas_call(
         functools.partial(kernel, n_z),
         out_shape=(pltpu.VMEM((rows_u, width), bf16), pltpu.VMEM((rows_i, width), bf16)),
@@ -306,12 +360,19 @@
             pltpu.VMEM((3, 3, 8, width), jnp.int32),
             pltpu.VMEM((blocks, rows_u, width), f32),
             pltpu.VMEM((blocks // 2, rows_u, width), f32),
-            pltpu.VMEM((n_z, rows_u, width), f32),
-            pltpu.VMEM((n_z, rows_u, width), f32),
+            pltpu.VMEM((n_z, rows_u, width), i16),
+            pltpu.VMEM((n_z, 8, width), f32),
+            pltpu.VMEM((n_z, rows_u, width), i16),
+            pltpu.VMEM((n_z, 8, width), f32),
             pltpu.VMEM(quarter, f32),
-            pltpu.VMEM(quarter, f32),
-            pltpu.VMEM(quarter, f32),
-            pltpu.VMEM(quarter, f32),
+            pltpu.VMEM(quarter, i16),
+            pltpu.VMEM((8, width), f32),
+            pltpu.VMEM(quarter, i16),
+            pltpu.VMEM((2, 8, width), f32),
+            pltpu.VMEM(quarter, i16),
+            pltpu.VMEM((4, 8, width), f32),
+            pltpu.VMEM(quarter, i16),
+            pltpu.VMEM((4, 8, width), f32),
             pltpu.SMEM((2,), jnp.int32),
             pltpu.SMEM((1, 1), jnp.int32),
             dma((5,)),

time: 22 us -> 20.3 us (0.923)
  Pallas kernels: 20.6 us -> 18.9 us
    pallas_call x1, Pallas kernels: 19.9 us -> 18.2 us  [planned(): pl.pallas_call(functools.partial(kernel, n_z), out_shape=(pltpu.VMEM((row...]
where the time goes in v1:
time: 20.3 us; the launch traced here: 20.2 us
  Pallas kernels  18.9 us (93%)
  between operations  1.29 us (6%)
    pallas_call x1, Pallas kernels, planned(): pl.pallas_call(functools.partial(kernel, n_z), out_shape=(pltpu.VMEM((row...  18.2 us
    pallas_call x1, Pallas kernels, planned(): pl.pallas_call(put, out_shape=[jax.ShapeDtypeStruct(out.shape, out.dtype)...  0.69 us

profile of v1, /device:TPU:1, one launch (start us, length us, event | category | flops | bytes accessed | tf_op | source)
XLA Modules:
  0.0 20.2 jit_solution(6334865492359256164)
XLA Ops:
  1.3 18.2 %shard_map.68 = (bf16[128,128]{1,0:T(8,128)(2,1)S(1)}, bf16[512,128]{1,0:T(8,128)(2,1)S(1)}) custom-call(s32[2]{0:T(128)} %bitcast.3, s32[1,1]{1,0:T(1,128)S(6)} %copy.7.count_in, bf16[128,128]{1,0:T(8,128)(2,1)} %user_in.1, bf16[512,128]{1,0:T(8,128)(2,1)} %item_in.1, bf16[4,128,512]{2,1,0:T(8,128)(2,1)} %bitcast.2), custom_call_target="tpu_custom_call" | custom-call | tf_op jit(solution)/shard_map/pallas_call | solution.py:349
  19.5 0.7 %shard_map.69 = (bf16[128,128]{1,0:T(8,128)(2,1)}, bf16[512,128]{1,0:T(8,128)(2,1)}) custom-call(bf16[128,128]{1,0:T(8,128)(2,1)S(1)} %get-tuple-element.4.users, bf16[512,128]{1,0:T(8,128)(2,1)S(1)} %get-tuple-element.5.items), custom_call_target="tpu_custom_call" | custom-call | tf_op jit(solution)/shard_map/pallas_call | solution.py:389

commit v2 on v1

v2 whole, which is shorter than its diff:
```python
import functools
import math

import jax
import jax.numpy as jnp
from jax import lax
from jax.experimental import pallas as pl
from jax.experimental.pallas import tpu as pltpu
from jax.sharding import PartitionSpec as P

MESH = pl.DeviceIdType.MESH
STEPS = 32760.0
TINY = 1e-30


def gathered(user_feats, item_feats, tile_values, tile_coords, tile_count):
    user_block = lax.all_gather(user_feats, "col", axis=0, tiled=True)
    item_block = lax.all_gather(item_feats, "row", axis=0, tiled=True)
    tiles = tile_values[0, 0]
    coords = tile_coords[0, 0]
    count = tile_count[0, 0]
    slots = tiles.shape[0]
    size = tiles.shape[1]
    width = user_block.shape[1]
    user_tiles = user_block.shape[0] // size
    item_tiles = item_block.shape[0] // size
    live = jnp.arange(slots) < count
    pick_user = ((coords[0][:, None] == jnp.arange(user_tiles)[None, :]) & live[:, None]).astype(
        jnp.bfloat16
    )
    pick_item = (coords[1][:, None] == jnp.arange(item_tiles)[None, :]).astype(jnp.bfloat16)
    user_sel = jnp.einsum(
        "su,uiw->siw",
        pick_user,
        user_block.reshape(user_tiles, size, width),
        preferred_element_type=jnp.float32,
    ).astype(jnp.bfloat16)
    item_sel = jnp.einsum(
        "st,tjw->sjw",
        pick_item,
        item_block.reshape(item_tiles, size, width),
        preferred_element_type=jnp.float32,
    ).astype(jnp.bfloat16)
    to_users = jnp.einsum("sij,sjw->siw", tiles, item_sel, preferred_element_type=jnp.float32)
    to_items = jnp.einsum("sij,siw->sjw", tiles, user_sel, preferred_element_type=jnp.float32)
    part_users = jnp.einsum(
        "su,siw->uiw", pick_user.astype(jnp.float32), to_users, precision=lax.Precision.HIGHEST
    ).reshape(user_tiles * size, width)
    part_items = jnp.einsum(
        "st,sjw->tjw", pick_item.astype(jnp.float32), to_items, precision=lax.Precision.HIGHEST
    ).reshape(item_tiles * size, width)
    users_next = lax.psum_scatter(part_users, "col", scatter_dimension=0, tiled=True)
    items_next = lax.psum_scatter(part_items, "row", scatter_dimension=0, tiled=True)
    return (users_next.astype(jnp.bfloat16), items_next.astype(jnp.bfloat16))


def encode(values):
    rows, width = values.shape
    groups = values.reshape(rows // 8, 8, width)
    peak = jnp.maximum(jnp.max(jnp.abs(groups), axis=0), TINY)
    return encode_by(values, peak), peak


def encode_by(values, peak):
    rows, width = values.shape
    groups = values.reshape(rows // 8, 8, width)
    scaled = jnp.round(groups * (STEPS / peak)[None])
    return scaled.astype(jnp.int32).astype(jnp.int16).reshape(rows, width)


def decode(code, peak):
    rows, width = code.shape
    groups = code.astype(jnp.int32).astype(jnp.float32).reshape(rows // 8, 8, width)
    return (groups * (peak * (1.0 / STEPS))[None]).reshape(rows, width)


def kernel(
    n_z,
    coords_in,
    count_in,
    user_in,
    item_in,
    tile_in,
    out_u,
    out_i,
    u_all,
    i_got,
    r_own,
    r_near,
    s_sel,
    tile_v,
    tile_t,
    meta,
    metas,
    part_u,
    from_p,
    send_z,
    peak_z,
    from_z,
    from_zp,
    part_i,
    send_1,
    peak_1,
    from_1,
    from_1p,
    pair_1,
    pair_1p,
    fwd_1,
    mask_1p,
    fwd_1p,
    send_2,
    peak_2,
    from_2,
    from_2p,
    gauge,
    coords,
    count,
    load_sem,
    sent,
    meta_r,
    uz_r,
    up_r,
    io_r,
    iq_r,
    ig_r,
    rp_r,
    rz_r,
    r1_r,
    rq_r,
    rf_r,
    r2_r,
):
    row, col = lax.axis_index("row"), lax.axis_index("col")
    y, x = row // 2, row % 2
    z, core = col // 2, col % 2
    row_x, row_y = 2 * y + 1 - x, 2 * (1 - y) + x
    twin = 2 * z + 1 - core
    x_dev, y_dev, p_dev = (row_x, twin), (row_y, twin), (row, twin)
    high = z // (n_z // 2)

    def far_first(at):
        mirrored = z + high * (n_z - 1 - 2 * z)
        to = n_z - 1 - at
        to = jnp.where(to <= mirrored, to - 1, to)
        return to + high * (n_z - 1 - 2 * to)

    others = [far_first(at) for at in range(n_z - 1)]
    z_devs = [(row, 2 * at + 1 - core) for at in others]
    near_first = others[::-1]
    rows_u, rows_i = user_in.shape[0], i_got.shape[0] * i_got.shape[2]
    size = tile_v.shape[-1]
    width = user_in.shape[1]
    half, chunk = rows_i // 2, rows_i // 4
    pieces = size // rows_u // 2
    order = (0, 2, 1, 3)
    sizes = []

    def user_slot(at):
        blocks = size // rows_u
        inner = pl.multiple_of(at % blocks * rows_u, rows_u)
        return u_all.at[at // blocks, pl.ds(inner, rows_u)]

    def quarter(c):
        return pl.ds(c % 2 * chunk, chunk)

    def send(src, dst, recv, device):
        sizes.append(math.prod(src.shape) * src.dtype.itemsize)
        copy(src, dst, sent.at[0], recv, device).start()

    def copy(src, dst, sem, recv, device):
        return pltpu.make_async_remote_copy(
            src_ref=src,
            dst_ref=dst,
            send_sem=sem,
            recv_sem=recv,
            device_id=device,
            device_id_type=MESH,
        )

    def arrived(like, recv):
        copy(like, like, recv, recv, x_dev).wait_recv()

    def landed(recv, *likes):
        total = sum(math.prod(like.shape) * like.dtype.itemsize for like in likes)
        arrived(gauge.at[pl.ds(0, total // (4 * width))], recv)

    barrier = pltpu.get_barrier_semaphore()
    peers = [x_dev, y_dev, p_dev] + z_devs
    for peer in peers:
        pl.semaphore_signal(barrier, inc=1, device_id=peer, device_id_type=MESH)
    loads = [
        pltpu.make_async_copy(user_in, user_slot(col), load_sem.at[0]),
        pltpu.make_async_copy(item_in, i_got.at[:, 0], load_sem.at[1]),
        pltpu.make_async_copy(tile_in, tile_v, load_sem.at[2]),
        pltpu.make_async_copy(coords_in, coords, load_sem.at[3]),
        pltpu.make_async_copy(count_in, count, load_sem.at[4]),
    ]
    for load in loads:
        load.start()

    loads[3].wait()
    loads[4].wait()
    tu, ti = coords[0], coords[1]
    meta[0] = jnp.full(meta.shape[1:], tu, jnp.int32)
    meta[1] = jnp.full(meta.shape[1:], ti, jnp.int32)
    my_tu, my_ti = meta[0][0:1, :], meta[1][0:1, :]
    live = jnp.full((1, width), count[0, 0], jnp.int32) > 0
    pl.semaphore_wait(barrier, len(peers))

    loads[0].wait()
    own = user_slot(col)
    for device in z_devs:
        send(own, own, uz_r.at[z], device)
    for at, device in enumerate((x_dev, y_dev, p_dev)):
        send(meta, metas.at[at], meta_r.at[0], device)
    loads[1].wait()
    for c in order:
        send(
            i_got.at[c // 2, 0, quarter(c)],
            r_near.at[c // 2, quarter(c)],
            iq_r.at[c],
            x_dev if c < 2 else y_dev,
        )
    send(own, own, up_r.at[0], p_dev)
    for part in range(2):
        send(i_got.at[part, 0], r_own.at[part], io_r.at[0], p_dev)

    loads[2].wait()
    tile_t[...] = tile_v[...].reshape(size, size).T
    arrived(metas, meta_r.at[0])
    x_ti, y_ti, p_ti = (metas[at, 1][0:1, :] for at in range(3))
    p_tu = metas[2, 0][0:1, :]
    arrived(r_own, io_r.at[0])

    def pass_user(at):
        slot = user_slot(2 * at + 1 - core)
        arrived(slot, uz_r.at[at])
        copy(slot, slot, sent.at[0], up_r.at[0], p_dev).start()

    def pass_items(c):
        part, want, near, device = (
            (0, y_ti, row_x, y_dev) if c < 2 else (1, x_ti, row_y, x_dev)
        )
        here = r_near.at[part, quarter(c)]
        arrived(here, iq_r.at[c])
        s_sel[part, quarter(c)] = jnp.where(
            want == near, r_near[part, quarter(c)], r_own[part, quarter(c)]
        )
        copy(
            s_sel.at[part, quarter(c)],
            i_got.at[part, 2, quarter(c)],
            sent.at[0],
            ig_r.at[0],
            device,
        ).start()
        copy(here, i_got.at[part, 1, quarter(c)], sent.at[0], ig_r.at[0], p_dev).start()

    users = [(pass_user, at) for at in near_first]
    items = [(pass_items, c) for c in order]
    sizes.extend([rows_u * width * 2] * len(users) + [chunk * width * 2] * (2 * len(items)))

    for step, at in users[:-1] + items + users[-1:]:
        step(at)

    arrived(u_all.at[pl.ds(0, u_all.shape[0] // 2)], up_r.at[0])

    user_sel = u_all[tu]
    user_sel = jnp.where(live, user_sel, 0.0).astype(user_sel.dtype)
    product_i = jnp.dot(tile_t[...], user_sel, preferred_element_type=jnp.float32)
    code, peak = encode(product_i)
    peak_1[...] = peak
    send_1[...] = code.reshape(send_1.shape)
    for at, device in enumerate((x_dev, y_dev)):
        send(peak_1, from_1p.at[at], r1_r.at[2 * at], device)
    for c in order:
        send(send_1.at[c], from_1.at[c], r1_r.at[c], x_dev if c < 2 else y_dev)
    send(peak_1, pair_1p, rq_r.at[0], p_dev)
    send(send_1, pair_1, rq_r.at[0], p_dev)
    part_i[...] = product_i.reshape(part_i.shape)

    arrived(i_got.at[:, pl.ds(1, 2)], ig_r.at[0])
    sel_x = jnp.where(ti == row, 0, jnp.where(ti == row_x, 1, 2))
    sel_y = jnp.where(ti == row, 0, jnp.where(ti == row_y, 1, 2))
    item_sel = jnp.concatenate([i_got[0, sel_x], i_got[1, sel_y]], axis=0)
    item_sel = jnp.where(live, item_sel, 0.0).astype(item_sel.dtype)

    def multiply(owner):
        rows = jnp.concatenate([tile_v[2 * h + owner] for h in range(pieces)], axis=0)
        product = jnp.dot(rows, item_sel, preferred_element_type=jnp.float32)
        for h in range(pieces):
            part_u[2 * h + owner] = product[h * rows_u : (h + 1) * rows_u]

    multiply(core)
    for h in range(pieces):
        send(part_u.at[2 * h + core], from_p.at[h], rp_r.at[0], p_dev)
    multiply(1 - core)

    def users_out():
        arrived(from_p, rp_r.at[0])
        for at, device in list(zip(others, z_devs)) + [(z, p_dev)]:
            tile, h = at // pieces, at % pieces
            send_z[at], peak_z[at] = encode(
                jnp.where(my_tu == tile, part_u[2 * h + 1 - core], 0.0)
                + jnp.where(p_tu == tile, from_p[h], 0.0)
            )
            copy(peak_z.at[at], from_zp.at[z], sent.at[0], rz_r.at[0], device).start()
            copy(send_z.at[at], from_z.at[z], sent.at[0], rz_r.at[0], device).start()

    def items_out():
        landed(rq_r.at[0], pair_1, pair_1p)
        for c in order:
            other, owner, device = (
                (x_ti, row_y, y_dev) if c < 2 else (y_ti, row_x, x_dev)
            )
            at = c // 2
            if c % 2 == 0:
                landed(r1_r.at[c], from_1.at[c], peak_1)
                mask_1p[at] = jnp.where(other == row, from_1p[at], 0.0)
                copy(mask_1p.at[at], fwd_1p.at[at], sent.at[0], rf_r.at[0], p_dev).start()
            else:
                arrived(from_1.at[c], r1_r.at[c])
            send_2[c], peak_2[c] = encode(
                jnp.where(p_ti == owner, decode(pair_1[c], pair_1p[...]), 0.0)
                + jnp.where(other == owner, decode(from_1[c], from_1p[at]), 0.0)
            )
            copy(peak_2.at[c], from_2p.at[c], sent.at[0], r2_r.at[c % 2], device).start()
            copy(send_2.at[c], from_2.at[c], sent.at[0], r2_r.at[c % 2], device).start()
            copy(from_1.at[c], fwd_1.at[c], sent.at[0], rf_r.at[0], p_dev).start()

    for ref in (peak_z, send_z, mask_1p, peak_2, send_2, from_1):
        sizes.append(math.prod(ref.shape) * ref.dtype.itemsize)

    users_out()
    items_out()

    landed(rf_r.at[0], fwd_1, fwd_1p)
    for c in order:
        if c in (0, 1):
            landed(r2_r.at[c % 2], from_2.at[pl.ds(0, 2)], from_2p.at[pl.ds(0, 2)])
        last = jnp.where(my_ti == row, part_i[c], 0.0) + decode(fwd_1[c], fwd_1p[c // 2])
        last = last + decode(from_2[c], from_2p[c])
        out_i[pl.ds(c * chunk, chunk), :] = last.astype(out_i.dtype)

    landed(rz_r.at[0], from_z, from_zp)
    total = decode(from_z[0], from_zp[0])
    for at in range(1, n_z):
        total = total + decode(from_z[at], from_zp[at])
    out_u[...] = total.astype(out_u.dtype)

    like = gauge.at[pl.ds(0, sum(sizes) // (4 * width))]
    copy(like, like, sent.at[0], sent.at[0], x_dev).wait_send()


def put(users, items, out_u, out_i, sems):
    copies = [
        pltpu.make_async_copy(users, out_u, sems.at[0]),
        pltpu.make_async_copy(items, out_i, sems.at[1]),
    ]
    for c in copies:
        c.start()
    for c in copies:
        c.wait()


def planned(user_feats, item_feats, tile_values, tile_coords, tile_count, *, n_z):
    rows_u, width = user_feats.shape
    rows_i = item_feats.shape[0]
    size = tile_values.shape[-1]
    f32, bf16, dma = jnp.float32, jnp.bfloat16, pltpu.SemaphoreType.DMA
    blocks = size // rows_u
    vmem = pl.BlockSpec(memory_space=pltpu.VMEM)
    anywhere = pl.BlockSpec(memory_space=pl.ANY)
    quarter = (4, rows_i // 4, width)
    peak = (8, width)
    i16 = jnp.int16
    vm = pltpu.VMEM
    outs = pl.pallas_call(
        functools.partial(kernel, n_z),
        out_shape=(pltpu.VMEM((rows_u, width), bf16), pltpu.VMEM((rows_i, width), bf16)),
        in_specs=[anywhere] * 5,
        out_specs=(vmem, vmem),
        scratch_shapes=[
            vm((2 * n_z * rows_u // size, size, width), bf16),
            vm((2, 3, rows_i // 2, width), bf16),
            vm((2, rows_i // 2, width), bf16),
            vm((2, rows_i // 2, width), bf16),
            vm((2, rows_i // 2, width), bf16),
            vm((blocks, rows_u, size), bf16),
            vm((size, size), bf16),
            vm((2,) + peak, jnp.int32),
            vm((3, 2) + peak, jnp.int32),
            vm((blocks, rows_u, width), f32),
            vm((blocks // 2, rows_u, width), f32),
            vm((n_z, rows_u, width), i16),
            vm((n_z,) + peak, f32),
            vm((n_z, rows_u, width), i16),
            vm((n_z,) + peak, f32),
            vm(quarter, f32),
            vm(quarter, i16),
            vm(peak, f32),
            vm(quarter, i16),
            vm((2,) + peak, f32),
            vm(quarter, i16),
            vm(peak, f32),
            vm(quarter, i16),
            vm((2,) + peak, f32),
            vm((2,) + peak, f32),
            vm(quarter, i16),
            vm((4,) + peak, f32),
            vm(quarter, i16),
            vm((4,) + peak, f32),
            vm((16 * rows_i, width), f32),
            pltpu.SMEM((2,), jnp.int32),
            pltpu.SMEM((1, 1), jnp.int32),
        ]
        + [dma((n,)) for n in (5, 1, 1, n_z, 1, 1, 4, 1, 1, 1, 4, 1, 1, 2)],
        compiler_params=pltpu.CompilerParams(collective_id=0, has_side_effects=True),
    )(
        tile_coords.reshape(2),
        tile_count,
        user_feats,
        item_feats.reshape(2, rows_i // 2, width),
        tile_values.reshape(blocks, rows_u, size),
    )
    return pl.pallas_call(
        put,
        out_shape=[jax.ShapeDtypeStruct(out.shape, out.dtype) for out in outs],
        in_specs=[vmem, vmem],
        out_specs=[anywhere, anywhere],
        scratch_shapes=[dma((2,))],
    )(*[pltpu.with_memory_space_constraint(out, pltpu.VMEM) for out in outs])


def solution(mesh):
    n_row, n_col = mesh.shape["row"], mesh.shape["col"]

    def local(user_feats, item_feats, tile_values, tile_coords, tile_count):
        slots, size = tile_values.shape[2], tile_values.shape[3]
        rows_u = user_feats.shape[0]
        fits = (
            n_row == 4
            and n_col % 2 == 0
            and slots == 1
            and item_feats.shape[0] == size
            and size % (2 * rows_u) == 0
            and n_col * rows_u % (2 * size) == 0
            and (n_col // 2 - 1) * rows_u <= size
        )
        args = (user_feats, item_feats, tile_values, tile_coords, tile_count)
        return planned(*args, n_z=n_col // 2) if fits else gathered(*args)

    placed = (
        P(("row", "col"), None),
        P(("col", "row"), None),
        P("row", "col", None, None, None),
        P("row", "col", None, None),
        P("row", "col"),
    )
    return jax.shard_map(
        local,
        mesh=mesh,
        in_specs=placed,
        out_specs=(P(("row", "col"), None), P(("col", "row"), None)),
        check_vma=False,
    )
```

time: 20.3 us -> 20.2 us (level)
  Pallas kernels: 18.9 us -> 18.6 us
    pallas_call x1, Pallas kernels: 18.2 us -> 17.9 us  [planned(): pl.pallas_call(functools.partial(kernel, n_z), out_shape=(pltpu.VMEM((row...]
where the time goes in v2:
time: 20.2 us; the launch traced here: 19.9 us
  Pallas kernels  18.6 us (92%)
  between operations  1.29 us (6%)
    pallas_call x1, Pallas kernels, planned(): pl.pallas_call(functools.partial(kernel, n_z), out_shape=(pltpu.VMEM((row...  17.9 us
    pallas_call x1, Pallas kernels, planned(): pl.pallas_call(put, out_shape=[jax.ShapeDtypeStruct(out.shape, out.dtype)...  0.69 us

profile of v2, /device:TPU:1, one launch (start us, length us, event | category | flops | bytes accessed | tf_op | source)
XLA Modules:
  0.0 19.9 jit_solution(13886798732742998663)
XLA Ops:
  1.3 17.9 %shard_map.68 = (bf16[128,128]{1,0:T(8,128)(2,1)S(1)}, bf16[512,128]{1,0:T(8,128)(2,1)S(1)}) custom-call(s32[2]{0:T(128)} %bitcast.5, s32[1,1]{1,0:T(1,128)S(6)} %copy.7.count_in, bf16[128,128]{1,0:T(8,128)(2,1)} %user_in.1, bf16[2,256,128]{2,1,0:T(8,128)(2,1)} %bitcast.4, bf16[4,128,512]{2,1,0:T(8,128)(2,1)} %bitcast.3), custom_call_target="tpu_custom_call" | custom-call | tf_op jit(solution)/shard_map/pallas_call | solution.py:377
  19.2 0.7 %shard_map.69 = (bf16[128,128]{1,0:T(8,128)(2,1)}, bf16[512,128]{1,0:T(8,128)(2,1)}) custom-call(bf16[128,128]{1,0:T(8,128)(2,1)S(1)} %get-tuple-element.4.users, bf16[512,128]{1,0:T(8,128)(2,1)S(1)} %get-tuple-element.5.items), custom_call_target="tpu_custom_call" | custom-call | tf_op jit(solution)/shard_map/pallas_call | solution.py:425

commit v3 on v2

--- a/solution.py
+++ b/solution.py
@@ -9,7 +9,8 @@
 from jax.sharding import PartitionSpec as P
 
 MESH = pl.DeviceIdType.MESH
-STEPS = 32760.0
+LEVELS = 32760.0
+STEPS = 4
 TINY = 1e-30
 
 
@@ -64,14 +65,14 @@
 def encode_by(values, peak):
     rows, width = values.shape
     groups = values.reshape(rows // 8, 8, width)
-    scaled = jnp.round(groups * (STEPS / peak)[None])
+    scaled = jnp.round(groups * (LEVELS / peak)[None])
     return scaled.astype(jnp.int32).astype(jnp.int16).reshape(rows, width)
 
 
 def decode(code, peak):
     rows, width = code.shape
     groups = code.astype(jnp.int32).astype(jnp.float32).reshape(rows // 8, 8, width)
-    return (groups * (peak * (1.0 / STEPS))[None]).reshape(rows, width)
+    return (groups * (peak * (1.0 / LEVELS))[None]).reshape(rows, width)
 
 
 def kernel(
@@ -117,6 +118,8 @@
     count,
     load_sem,
     sent,
+    first_s,
+    late,
     meta_r,
     uz_r,
     up_r,
@@ -150,9 +153,9 @@
     rows_u, rows_i = user_in.shape[0], i_got.shape[0] * i_got.shape[2]
     size = tile_v.shape[-1]
     width = user_in.shape[1]
-    half, chunk = rows_i // 2, rows_i // 4
+    steps = send_1.shape[1]
+    chunk = rows_i // (2 * steps)
     pieces = size // rows_u // 2
-    order = (0, 2, 1, 3)
     sizes = []
 
     def user_slot(at):
@@ -160,8 +163,8 @@
         inner = pl.multiple_of(at % blocks * rows_u, rows_u)
         return u_all.at[at // blocks, pl.ds(inner, rows_u)]
 
-    def quarter(c):
-        return pl.ds(c % 2 * chunk, chunk)
+    def rows_of(step):
+        return pl.ds(step * chunk, chunk)
 
     def send(src, dst, recv, device):
         sizes.append(math.prod(src.shape) * src.dtype.itemsize)
@@ -185,9 +188,16 @@
         arrived(gauge.at[pl.ds(0, total // (4 * width))], recv)
 
     barrier = pltpu.get_barrier_semaphore()
-    peers = [x_dev, y_dev, p_dev] + z_devs
+    across, mates = z_devs[: n_z // 2], z_devs[n_z // 2 :]
+    peers = [x_dev, y_dev, p_dev] + mates
     for peer in peers:
         pl.semaphore_signal(barrier, inc=1, device_id=peer, device_id_type=MESH)
+
+    @pl.when(high == 0)
+    def _():
+        for peer in across:
+            pl.semaphore_signal(barrier, inc=1, device_id=peer, device_id_type=MESH)
+
     loads = [
         pltpu.make_async_copy(user_in, user_slot(col), load_sem.at[0]),
         pltpu.make_async_copy(item_in, i_got.at[:, 0], load_sem.at[1]),
@@ -205,28 +215,43 @@
     meta[1] = jnp.full(meta.shape[1:], ti, jnp.int32)
     my_tu, my_ti = meta[0][0:1, :], meta[1][0:1, :]
     live = jnp.full((1, width), count[0, 0], jnp.int32) > 0
-    pl.semaphore_wait(barrier, len(peers))
+    pl.semaphore_wait(barrier, len(peers) + high * len(across))
 
     loads[0].wait()
     own = user_slot(col)
-    for device in z_devs:
+
+    @pl.when(high == 1)
+    def _():
+        for peer in across:
+            pl.semaphore_signal(late, inc=1, device_id=peer, device_id_type=MESH)
+        copy(own, own, first_s.at[0], uz_r.at[z], across[0]).start()
+
+    sizes.extend([rows_u * width * 2] * (len(across) - 1))
+    for device in mates:
         send(own, own, uz_r.at[z], device)
     for at, device in enumerate((x_dev, y_dev, p_dev)):
         send(meta, metas.at[at], meta_r.at[0], device)
     loads[1].wait()
-    for c in order:
-        send(
-            i_got.at[c // 2, 0, quarter(c)],
-            r_near.at[c // 2, quarter(c)],
-            iq_r.at[c],
-            x_dev if c < 2 else y_dev,
-        )
+    for step in range(steps):
+        for part, device in ((0, x_dev), (1, y_dev)):
+            send(
+                i_got.at[part, 0, rows_of(step)],
+                r_near.at[part, rows_of(step)],
+                iq_r.at[step],
+                device,
+            )
     send(own, own, up_r.at[0], p_dev)
     for part in range(2):
         send(i_got.at[part, 0], r_own.at[part], io_r.at[0], p_dev)
 
     loads[2].wait()
     tile_t[...] = tile_v[...].reshape(size, size).T
+    @pl.when(high == 1)
+    def _():
+        copy(own, own, first_s.at[0], uz_r.at[z], across[0]).wait_send()
+        for device in across[1:]:
+            copy(own, own, sent.at[0], uz_r.at[z], device).start()
+
     arrived(metas, meta_r.at[0])
     x_ti, y_ti, p_ti = (metas[at, 1][0:1, :] for at in range(3))
     p_tu = metas[2, 0][0:1, :]
@@ -237,63 +262,84 @@
         arrived(slot, uz_r.at[at])
         copy(slot, slot, sent.at[0], up_r.at[0], p_dev).start()
 
-    def pass_items(c):
-        part, want, near, device = (
-            (0, y_ti, row_x, y_dev) if c < 2 else (1, x_ti, row_y, x_dev)
-        )
-        here = r_near.at[part, quarter(c)]
-        arrived(here, iq_r.at[c])
-        s_sel[part, quarter(c)] = jnp.where(
-            want == near, r_near[part, quarter(c)], r_own[part, quarter(c)]
-        )
-        copy(
-            s_sel.at[part, quarter(c)],
-            i_got.at[part, 2, quarter(c)],
-            sent.at[0],
-            ig_r.at[0],
-            device,
-        ).start()
-        copy(here, i_got.at[part, 1, quarter(c)], sent.at[0], ig_r.at[0], p_dev).start()
+    def pass_items(step):
+        landed(iq_r.at[step], r_near.at[:, rows_of(step)])
+        for part, want, near, device in ((0, y_ti, row_x, y_dev), (1, x_ti, row_y, x_dev)):
+            here = (part, rows_of(step))
+            s_sel[here] = jnp.where(want == near, r_near[here], r_own[here])
+            copy(
+                s_sel.at[here], i_got.at[part, 2, rows_of(step)], sent.at[0], ig_r.at[0], device
+            ).start()
+            copy(
+                r_near.at[here], i_got.at[part, 1, rows_of(step)], sent.at[0], ig_r.at[0], p_dev
+            ).start()
 
     users = [(pass_user, at) for at in near_first]
-    items = [(pass_items, c) for c in order]
-    sizes.extend([rows_u * width * 2] * len(users) + [chunk * width * 2] * (2 * len(items)))
-
-    for step, at in users[:-1] + items + users[-1:]:
+    items = [(pass_items, step) for step in range(steps)]
+    sizes.extend([rows_u * width * 2] * len(users) + [chunk * width * 2] * (4 * steps))
+
+    for step, at in users[: len(mates)]:
         step(at)
 
-    arrived(u_all.at[pl.ds(0, u_all.shape[0] // 2)], up_r.at[0])
-
-    user_sel = u_all[tu]
-    user_sel = jnp.where(live, user_sel, 0.0).astype(user_sel.dtype)
-    product_i = jnp.dot(tile_t[...], user_sel, preferred_element_type=jnp.float32)
-    code, peak = encode(product_i)
-    peak_1[...] = peak
-    send_1[...] = code.reshape(send_1.shape)
-    for at, device in enumerate((x_dev, y_dev)):
-        send(peak_1, from_1p.at[at], r1_r.at[2 * at], device)
-    for c in order:
-        send(send_1.at[c], from_1.at[c], r1_r.at[c], x_dev if c < 2 else y_dev)
-    send(peak_1, pair_1p, rq_r.at[0], p_dev)
-    send(send_1, pair_1, rq_r.at[0], p_dev)
-    part_i[...] = product_i.reshape(part_i.shape)
-
-    arrived(i_got.at[:, pl.ds(1, 2)], ig_r.at[0])
-    sel_x = jnp.where(ti == row, 0, jnp.where(ti == row_x, 1, 2))
-    sel_y = jnp.where(ti == row, 0, jnp.where(ti == row_y, 1, 2))
-    item_sel = jnp.concatenate([i_got[0, sel_x], i_got[1, sel_y]], axis=0)
-    item_sel = jnp.where(live, item_sel, 0.0).astype(item_sel.dtype)
-
-    def multiply(owner):
-        rows = jnp.concatenate([tile_v[2 * h + owner] for h in range(pieces)], axis=0)
-        product = jnp.dot(rows, item_sel, preferred_element_type=jnp.float32)
+    @pl.when(high == 0)
+    def _():
+        pl.semaphore_wait(late, len(across))
+        for device in across[:0:-1]:
+            copy(own, own, sent.at[0], uz_r.at[z], device).start()
+        copy(own, own, first_s.at[0], uz_r.at[z], across[0]).start()
+
+    for step, at in items + users[len(mates) :]:
+        step(at)
+
+    def users_product():
+        arrived(i_got.at[:, pl.ds(1, 2)], ig_r.at[0])
+        sel_x = jnp.where(ti == row, 0, jnp.where(ti == row_x, 1, 2))
+        sel_y = jnp.where(ti == row, 0, jnp.where(ti == row_y, 1, 2))
+        item_sel = jnp.concatenate([i_got[0, sel_x], i_got[1, sel_y]], axis=0)
+        item_sel = jnp.where(live, item_sel, 0.0).astype(item_sel.dtype)
+
+        def multiply(owner):
+            rows = jnp.concatenate([tile_v[2 * h + owner] for h in range(pieces)], axis=0)
+            product = jnp.dot(rows, item_sel, preferred_element_type=jnp.float32)
+            for h in range(pieces):
+                part_u[2 * h + owner] = product[h * rows_u : (h + 1) * rows_u]
+
+        multiply(core)
         for h in range(pieces):
-            part_u[2 * h + owner] = product[h * rows_u : (h + 1) * rows_u]
-
-    multiply(core)
-    for h in range(pieces):
-        send(part_u.at[2 * h + core], from_p.at[h], rp_r.at[0], p_dev)
-    multiply(1 - core)
+            copy(part_u.at[2 * h + core], from_p.at[h], sent.at[0], rp_r.at[0], p_dev).start()
+        multiply(1 - core)
+
+    def items_product():
+        arrived(u_all.at[pl.ds(0, u_all.shape[0] // 2)], up_r.at[0])
+
+        user_sel = u_all[tu]
+        user_sel = jnp.where(live, user_sel, 0.0).astype(user_sel.dtype)
+        product_i = jnp.dot(tile_t[...], user_sel, preferred_element_type=jnp.float32)
+        code, peak = encode(product_i)
+        peak_1[...] = peak
+        send_1[...] = code.reshape(send_1.shape)
+        for part, device in enumerate((x_dev, y_dev)):
+            copy(peak_1, from_1p.at[part], sent.at[0], r1_r.at[0], device).start()
+        for step in range(steps):
+            for part, device in enumerate((x_dev, y_dev)):
+                here = (part, step)
+                copy(send_1.at[here], from_1.at[here], sent.at[0], r1_r.at[step], device).start()
+        copy(peak_1, pair_1p, sent.at[0], rq_r.at[0], p_dev).start()
+        copy(send_1, pair_1, sent.at[0], rq_r.at[0], p_dev).start()
+        part_i[...] = product_i.reshape(part_i.shape)
+
+    for ref in (from_p, peak_1, peak_1, peak_1, send_1, send_1):
+        sizes.append(math.prod(ref.shape) * ref.dtype.itemsize)
+
+    @pl.when(high == 0)
+    def _():
+        items_product()
+        users_product()
+
+    @pl.when(high == 1)
+    def _():
+        users_product()
+        items_product()
 
     def users_out():
         arrived(from_p, rp_r.at[0])
@@ -308,24 +354,34 @@
 
     def items_out():
         landed(rq_r.at[0], pair_1, pair_1p)
-        for c in order:
-            other, owner, device = (
-                (x_ti, row_y, y_dev) if c < 2 else (y_ti, row_x, x_dev)
-            )
-            at = c // 2
-            if c % 2 == 0:
-                landed(r1_r.at[c], from_1.at[c], peak_1)
-                mask_1p[at] = jnp.where(other == row, from_1p[at], 0.0)
-                copy(mask_1p.at[at], fwd_1p.at[at], sent.at[0], rf_r.at[0], p_dev).start()
+        sides = ((0, x_ti, row_y, y_dev), (1, y_ti, row_x, x_dev))
+        for step in range(steps):
+            if step == 0:
+                landed(r1_r.at[0], from_1.at[:, 0], from_1p)
+                for part, other, owner, device in sides:
+                    mask_1p[part] = jnp.where(other == row, from_1p[part], 0.0)
+                    peak_2[part] = jnp.where(p_ti == owner, pair_1p[...], 0.0) + jnp.where(
+                        other == owner, from_1p[part], TINY
+                    )
+                    copy(
+                        peak_2.at[part], from_2p.at[part], sent.at[0], r2_r.at[0], device
+                    ).start()
             else:
-                arrived(from_1.at[c], r1_r.at[c])
-            send_2[c], peak_2[c] = encode(
-                jnp.where(p_ti == owner, decode(pair_1[c], pair_1p[...]), 0.0)
-                + jnp.where(other == owner, decode(from_1[c], from_1p[at]), 0.0)
-            )
-            copy(peak_2.at[c], from_2p.at[c], sent.at[0], r2_r.at[c % 2], device).start()
-            copy(send_2.at[c], from_2.at[c], sent.at[0], r2_r.at[c % 2], device).start()
-            copy(from_1.at[c], fwd_1.at[c], sent.at[0], rf_r.at[0], p_dev).start()
+                landed(r1_r.at[step], from_1.at[:, step])
+            for part, other, owner, device in sides:
+                here = (part, step)
+                send_2[here] = encode_by(
+                    jnp.where(p_ti == owner, decode(pair_1[here], pair_1p[...]), 0.0)
+                    + jnp.where(other == owner, decode(from_1[here], from_1p[part]), 0.0),
+                    peak_2[part],
+                )
+                copy(
+                    send_2.at[here], from_2.at[here], sent.at[0], r2_r.at[step], device
+                ).start()
+            for part in range(2):
+                here = (part, step)
+                copy(from_1.at[here], fwd_1.at[here], sent.at[0], rf_r.at[0], p_dev).start()
+        copy(mask_1p, fwd_1p, sent.at[0], rf_r.at[0], p_dev).start()
 
     for ref in (peak_z, send_z, mask_1p, peak_2, send_2, from_1):
         sizes.append(math.prod(ref.shape) * ref.dtype.itemsize)
@@ -334,18 +390,28 @@
     items_out()
 
     landed(rf_r.at[0], fwd_1, fwd_1p)
-    for c in order:
-        if c in (0, 1):
-            landed(r2_r.at[c % 2], from_2.at[pl.ds(0, 2)], from_2p.at[pl.ds(0, 2)])
-        last = jnp.where(my_ti == row, part_i[c], 0.0) + decode(fwd_1[c], fwd_1p[c // 2])
-        last = last + decode(from_2[c], from_2p[c])
-        out_i[pl.ds(c * chunk, chunk), :] = last.astype(out_i.dtype)
+    for step in range(steps):
+        if step == 0:
+            landed(r2_r.at[0], from_2.at[:, 0], from_2p)
+        else:
+            landed(r2_r.at[step], from_2.at[:, step])
+        for part in range(2):
+            here = (part, step)
+            last = jnp.where(my_ti == row, part_i[here], 0.0)
+            last = last + decode(fwd_1[here], fwd_1p[part])
+            last = last + decode(from_2[here], from_2p[part])
+            start = part * (rows_i // 2) + step * chunk
+            out_i[pl.ds(start, chunk), :] = last.astype(out_i.dtype)
 
     landed(rz_r.at[0], from_z, from_zp)
     total = decode(from_z[0], from_zp[0])
     for at in range(1, n_z):
         total = total + decode(from_z[at], from_zp[at])
     out_u[...] = total.astype(out_u.dtype)
+
+    @pl.when(high == 0)
+    def _():
+        copy(own, own, first_s.at[0], uz_r.at[z], across[0]).wait_send()
 
     like = gauge.at[pl.ds(0, sum(sizes) // (4 * width))]
     copy(like, like, sent.at[0], sent.at[0], x_dev).wait_send()
@@ -370,7 +436,7 @@
     blocks = size // rows_u
     vmem = pl.BlockSpec(memory_space=pltpu.VMEM)
     anywhere = pl.BlockSpec(memory_space=pl.ANY)
-    quarter = (4, rows_i // 4, width)
+    cut = (2, STEPS, rows_i // (2 * STEPS), width)
     peak = (8, width)
     i16 = jnp.int16
     vm = pltpu.VMEM
@@ -395,25 +461,27 @@
             vm((n_z,) + peak, f32),
             vm((n_z, rows_u, width), i16),
             vm((n_z,) + peak, f32),
-            vm(quarter, f32),
-            vm(quarter, i16),
+            vm(cut, f32),
+            vm(cut, i16),
             vm(peak, f32),
-            vm(quarter, i16),
+            vm(cut, i16),
             vm((2,) + peak, f32),
-            vm(quarter, i16),
+            vm(cut, i16),
             vm(peak, f32),
-            vm(quarter, i16),
+            vm(cut, i16),
             vm((2,) + peak, f32),
             vm((2,) + peak, f32),
-            vm(quarter, i16),
-            vm((4,) + peak, f32),
-            vm(quarter, i16),
-            vm((4,) + peak, f32),
+            vm(cut, i16),
+            vm((2,) + peak, f32),
+            vm(cut, i16),
+            vm((2,) + peak, f32),
             vm((16 * rows_i, width), f32),
             pltpu.SMEM((2,), jnp.int32),
             pltpu.SMEM((1, 1), jnp.int32),
         ]
-        + [dma((n,)) for n in (5, 1, 1, n_z, 1, 1, 4, 1, 1, 1, 4, 1, 1, 2)],
+        + [dma((n,)) for n in (5, 1, 1)]
+        + [pltpu.SemaphoreType.REGULAR]
+        + [dma((n,)) for n in (1, n_z, 1, 1, STEPS, 1, 1, 1, STEPS, 1, 1, STEPS)],
         compiler_params=pltpu.CompilerParams(collective_id=0, has_side_effects=True),
     )(
         tile_coords.reshape(2),
@@ -443,6 +511,7 @@
             and slots == 1
             and item_feats.shape[0] == size
             and size % (2 * rows_u) == 0
+            and size % (32 * STEPS) == 0
             and n_col * rows_u % (2 * size) == 0
             and (n_col // 2 - 1) * rows_u <= size
         )

time: 20.2 us -> 19.9 us (0.985)
    pallas_call x1, Pallas kernels: 17.9 us -> 17.7 us  [planned(): pl.pallas_call(functools.partial(kernel, n_z), out_shape=(pltpu.VMEM((row...]
where the time goes in v3:
time: 19.9 us; the launch traced here: 19.7 us
  Pallas kernels  18.4 us (92%)
  between operations  1.29 us (6%)
    pallas_call x1, Pallas kernels, planned(): pl.pallas_call(functools.partial(kernel, n_z), out_shape=(pltpu.VMEM((row...  17.7 us
    pallas_call x1, Pallas kernels, planned(): pl.pallas_call(put, out_shape=[jax.ShapeDtypeStruct(out.shape, out.dtype)...  0.69 us

profile of v3, /device:TPU:1, one launch (start us, length us, event | category | flops | bytes accessed | tf_op | source)
XLA Modules:
  0.0 19.7 jit_solution(10146275383989397798)
XLA Ops:
  1.3 17.7 %shard_map.68 = (bf16[128,128]{1,0:T(8,128)(2,1)S(1)}, bf16[512,128]{1,0:T(8,128)(2,1)S(1)}) custom-call(s32[2]{0:T(128)} %bitcast.5, s32[1,1]{1,0:T(1,128)S(6)} %copy.7.count_in, bf16[128,128]{1,0:T(8,128)(2,1)} %user_in.1, bf16[2,256,128]{2,1,0:T(8,128)(2,1)} %bitcast.4, bf16[4,128,512]{2,1,0:T(8,128)(2,1)} %bitcast.3), custom_call_target="tpu_custom_call" | custom-call | tf_op jit(solution)/shard_map/pallas_call | solution.py:443
  19.0 0.7 %shard_map.69 = (bf16[128,128]{1,0:T(8,128)(2,1)}, bf16[512,128]{1,0:T(8,128)(2,1)}) custom-call(bf16[128,128]{1,0:T(8,128)(2,1)S(1)} %get-tuple-element.4.users, bf16[512,128]{1,0:T(8,128)(2,1)S(1)} %get-tuple-element.5.items), custom_call_target="tpu_custom_call" | custom-call | tf_op jit(solution)/shard_map/pallas_call | solution.py:493

commit v4 on v3

--- a/solution.py
+++ b/solution.py
@@ -11,6 +11,7 @@
 MESH = pl.DeviceIdType.MESH
 LEVELS = 32760.0
 STEPS = 4
+GROUPS = 2
 TINY = 1e-30
 
 
@@ -115,12 +116,10 @@
     from_2p,
     gauge,
     coords,
-    count,
     load_sem,
     sent,
     first_s,
     late,
-    meta_r,
     uz_r,
     up_r,
     io_r,
@@ -130,7 +129,6 @@
     rz_r,
     r1_r,
     rq_r,
-    rf_r,
     r2_r,
 ):
     row, col = lax.axis_index("row"), lax.axis_index("col")
@@ -154,7 +152,9 @@
     size = tile_v.shape[-1]
     width = user_in.shape[1]
     steps = send_1.shape[1]
-    chunk = rows_i // (2 * steps)
+    groups = peak_1.shape[0]
+    half, each = rows_i // 2, steps // groups
+    chunk = half // steps
     pieces = size // rows_u // 2
     sizes = []
 
@@ -203,18 +203,16 @@
         pltpu.make_async_copy(item_in, i_got.at[:, 0], load_sem.at[1]),
         pltpu.make_async_copy(tile_in, tile_v, load_sem.at[2]),
         pltpu.make_async_copy(coords_in, coords, load_sem.at[3]),
-        pltpu.make_async_copy(count_in, count, load_sem.at[4]),
-    ]
+            ]
     for load in loads:
         load.start()
 
     loads[3].wait()
-    loads[4].wait()
     tu, ti = coords[0], coords[1]
     meta[0] = jnp.full(meta.shape[1:], tu, jnp.int32)
     meta[1] = jnp.full(meta.shape[1:], ti, jnp.int32)
     my_tu, my_ti = meta[0][0:1, :], meta[1][0:1, :]
-    live = jnp.full((1, width), count[0, 0], jnp.int32) > 0
+    live = jnp.full((1, width), count_in[0, 0], jnp.int32) > 0
     pl.semaphore_wait(barrier, len(peers) + high * len(across))
 
     loads[0].wait()
@@ -230,7 +228,7 @@
     for device in mates:
         send(own, own, uz_r.at[z], device)
     for at, device in enumerate((x_dev, y_dev, p_dev)):
-        send(meta, metas.at[at], meta_r.at[0], device)
+        send(meta, metas.at[at], io_r.at[0], device)
     loads[1].wait()
     for step in range(steps):
         for part, device in ((0, x_dev), (1, y_dev)):
@@ -252,10 +250,9 @@
         for device in across[1:]:
             copy(own, own, sent.at[0], uz_r.at[z], device).start()
 
-    arrived(metas, meta_r.at[0])
+    landed(io_r.at[0], metas, r_own)
     x_ti, y_ti, p_ti = (metas[at, 1][0:1, :] for at in range(3))
     p_tu = metas[2, 0][0:1, :]
-    arrived(r_own, io_r.at[0])
 
     def pass_user(at):
         slot = user_slot(2 * at + 1 - core)
@@ -288,8 +285,13 @@
             copy(own, own, sent.at[0], uz_r.at[z], device).start()
         copy(own, own, first_s.at[0], uz_r.at[z], across[0]).start()
 
-    for step, at in items + users[len(mates) :]:
+    for step, at in items:
         step(at)
+
+    def pass_across():
+        for step, at in users[len(mates) :]:
+            step(at)
+
 
     def users_product():
         arrived(i_got.at[:, pl.ds(1, 2)], ig_r.at[0])
@@ -314,36 +316,36 @@
 
         user_sel = u_all[tu]
         user_sel = jnp.where(live, user_sel, 0.0).astype(user_sel.dtype)
-        product_i = jnp.dot(tile_t[...], user_sel, preferred_element_type=jnp.float32)
-        code, peak = encode(product_i)
-        peak_1[...] = peak
-        send_1[...] = code.reshape(send_1.shape)
-        for part, device in enumerate((x_dev, y_dev)):
-            copy(peak_1, from_1p.at[part], sent.at[0], r1_r.at[0], device).start()
-        for step in range(steps):
+        for g in range(groups):
+            rows = g * chunk * each
+            lhs = [tile_t[part * half + rows : part * half + rows + chunk * each] for part in range(2)]
+            product = jnp.dot(
+                jnp.concatenate(lhs, axis=0), user_sel, preferred_element_type=jnp.float32
+            )
+            code, peak_1[g] = encode(product)
+            some = slice(g * each, (g + 1) * each)
+            send_1[:, some] = code.reshape(2, each, chunk, width)
             for part, device in enumerate((x_dev, y_dev)):
-                here = (part, step)
-                copy(send_1.at[here], from_1.at[here], sent.at[0], r1_r.at[step], device).start()
+                copy(
+                    peak_1.at[g], from_1p.at[part, g], sent.at[0], r1_r.at[g * each], device
+                ).start()
+            for step in range(g * each, (g + 1) * each):
+                for part, device in enumerate((x_dev, y_dev)):
+                    here = (part, step)
+                    copy(
+                        send_1.at[here], from_1.at[here], sent.at[0], r1_r.at[step], device
+                    ).start()
+            part_i[:, some] = product.reshape(2, each, chunk, width)
         copy(peak_1, pair_1p, sent.at[0], rq_r.at[0], p_dev).start()
         copy(send_1, pair_1, sent.at[0], rq_r.at[0], p_dev).start()
-        part_i[...] = product_i.reshape(part_i.shape)
 
     for ref in (from_p, peak_1, peak_1, peak_1, send_1, send_1):
         sizes.append(math.prod(ref.shape) * ref.dtype.itemsize)
 
-    @pl.when(high == 0)
-    def _():
-        items_product()
-        users_product()
-
-    @pl.when(high == 1)
-    def _():
-        users_product()
-        items_product()
-
     def users_out():
         arrived(from_p, rp_r.at[0])
-        for at, device in list(zip(others, z_devs)) + [(z, p_dev)]:
+        to = list(zip(others, z_devs))
+        for at, device in to[:1] + to[n_z // 2 :] + [(z, p_dev)] + to[1 : n_z // 2]:
             tile, h = at // pieces, at % pieces
             send_z[at], peak_z[at] = encode(
                 jnp.where(my_tu == tile, part_u[2 * h + 1 - core], 0.0)
@@ -356,51 +358,68 @@
         landed(rq_r.at[0], pair_1, pair_1p)
         sides = ((0, x_ti, row_y, y_dev), (1, y_ti, row_x, x_dev))
         for step in range(steps):
-            if step == 0:
-                landed(r1_r.at[0], from_1.at[:, 0], from_1p)
+            g = step // each
+            if step % each == 0:
+                landed(r1_r.at[step], from_1.at[:, step], from_1p.at[:, g])
                 for part, other, owner, device in sides:
-                    mask_1p[part] = jnp.where(other == row, from_1p[part], 0.0)
-                    peak_2[part] = jnp.where(p_ti == owner, pair_1p[...], 0.0) + jnp.where(
-                        other == owner, from_1p[part], TINY
+                    mask_1p[part, g] = jnp.where(other == row, from_1p[part, g], 0.0)
+                    peak_2[part, g] = jnp.where(p_ti == owner, pair_1p[g], 0.0) + jnp.where(
+                        other == owner, from_1p[part, g], TINY
                     )
                     copy(
-                        peak_2.at[part], from_2p.at[part], sent.at[0], r2_r.at[0], device
+                        peak_2.at[part, g], from_2p.at[part, g], sent.at[0], r2_r.at[step], device
                     ).start()
             else:
                 landed(r1_r.at[step], from_1.at[:, step])
             for part, other, owner, device in sides:
                 here = (part, step)
                 send_2[here] = encode_by(
-                    jnp.where(p_ti == owner, decode(pair_1[here], pair_1p[...]), 0.0)
-                    + jnp.where(other == owner, decode(from_1[here], from_1p[part]), 0.0),
-                    peak_2[part],
+                    jnp.where(p_ti == owner, decode(pair_1[here], pair_1p[g]), 0.0)
+                    + jnp.where(other == owner, decode(from_1[here], from_1p[part, g]), 0.0),
+                    peak_2[part, g],
                 )
                 copy(
                     send_2.at[here], from_2.at[here], sent.at[0], r2_r.at[step], device
                 ).start()
             for part in range(2):
                 here = (part, step)
-                copy(from_1.at[here], fwd_1.at[here], sent.at[0], rf_r.at[0], p_dev).start()
-        copy(mask_1p, fwd_1p, sent.at[0], rf_r.at[0], p_dev).start()
+                copy(from_1.at[here], fwd_1.at[here], sent.at[0], r2_r.at[0], p_dev).start()
+        copy(mask_1p, fwd_1p, sent.at[0], r2_r.at[0], p_dev).start()
 
     for ref in (peak_z, send_z, mask_1p, peak_2, send_2, from_1):
         sizes.append(math.prod(ref.shape) * ref.dtype.itemsize)
 
-    users_out()
-    items_out()
-
-    landed(rf_r.at[0], fwd_1, fwd_1p)
+    @pl.when(high == 0)
+    def _():
+        pass_across()
+        items_product()
+        users_product()
+        users_out()
+        items_out()
+
+    @pl.when(high == 1)
+    def _():
+        pass_across()
+        users_product()
+        items_product()
+        users_out()
+        items_out()
+
+
     for step in range(steps):
+        g = step // each
         if step == 0:
-            landed(r2_r.at[0], from_2.at[:, 0], from_2p)
+            landed(r2_r.at[0], from_2.at[:, 0], from_2p.at[:, 0], fwd_1, fwd_1p)
+        elif step % each == 0:
+            landed(r2_r.at[step], from_2.at[:, step], from_2p.at[:, g])
         else:
             landed(r2_r.at[step], from_2.at[:, step])
         for part in range(2):
             here = (part, step)
             last = jnp.where(my_ti == row, part_i[here], 0.0)
-            last = last + decode(fwd_1[here], fwd_1p[part])
-            last = last + decode(from_2[here], from_2p[part])
-            start = part * (rows_i // 2) + step * chunk
+            last = last + decode(fwd_1[here], fwd_1p[part, g])
+            last = last + decode(from_2[here], from_2p[part, g])
+            start = part * half + step * chunk
             out_i[pl.ds(start, chunk), :] = last.astype(out_i.dtype)
 
     landed(rz_r.at[0], from_z, from_zp)
@@ -443,7 +462,7 @@
     outs = pl.pallas_call(
         functools.partial(kernel, n_z),
         out_shape=(pltpu.VMEM((rows_u, width), bf16), pltpu.VMEM((rows_i, width), bf16)),
-        in_specs=[anywhere] * 5,
+        in_specs=[anywhere, pl.BlockSpec(memory_space=pltpu.SMEM)] + [anywhere] * 3,
         out_specs=(vmem, vmem),
         scratch_shapes=[
             vm((2 * n_z * rows_u // size, size, width), bf16),
@@ -463,25 +482,24 @@
             vm((n_z,) + peak, f32),
             vm(cut, f32),
             vm(cut, i16),
-            vm(peak, f32),
+            vm((GROUPS,) + peak, f32),
             vm(cut, i16),
-            vm((2,) + peak, f32),
+            vm((2, GROUPS) + peak, f32),
             vm(cut, i16),
-            vm(peak, f32),
+            vm((GROUPS,) + peak, f32),
             vm(cut, i16),
-            vm((2,) + peak, f32),
-            vm((2,) + peak, f32),
+            vm((2, GROUPS) + peak, f32),
+            vm((2, GROUPS) + peak, f32),
             vm(cut, i16),
-            vm((2,) + peak, f32),
+            vm((2, GROUPS) + peak, f32),
             vm(cut, i16),
-            vm((2,) + peak, f32),
+            vm((2, GROUPS) + peak, f32),
             vm((16 * rows_i, width), f32),
             pltpu.SMEM((2,), jnp.int32),
-            pltpu.SMEM((1, 1), jnp.int32),
         ]
-        + [dma((n,)) for n in (5, 1, 1)]
+        + [dma((n,)) for n in (4, 1, 1)]
         + [pltpu.SemaphoreType.REGULAR]
-        + [dma((n,)) for n in (1, n_z, 1, 1, STEPS, 1, 1, 1, STEPS, 1, 1, STEPS)],
+        + [dma((n,)) for n in (n_z, 1, 1, STEPS, 1, 1, 1, STEPS, 1, STEPS)],
         compiler_params=pltpu.CompilerParams(collective_id=0, has_side_effects=True),
     )(
         tile_coords.reshape(2),

time: 19.9 us -> 19.8 us (level)
  no operation moved by 1% of the time
where the time goes in v4:
time: 19.8 us; the launch traced here: 19.6 us
  Pallas kernels  18.4 us (93%)
  between operations  1.29 us (7%)
    pallas_call x1, Pallas kernels, planned(): pl.pallas_call(functools.partial(kernel, n_z), out_shape=(pltpu.VMEM((row...  17.7 us
    pallas_call x1, Pallas kernels, planned(): pl.pallas_call(put, out_shape=[jax.ShapeDtypeStruct(out.shape, out.dtype)...  0.69 us

profile of v4, /device:TPU:1, one launch (start us, length us, event | category | flops | bytes accessed | tf_op | source)
XLA Modules:
  0.0 19.6 jit_solution(7374616552762034112)
XLA Ops:
  1.3 17.7 %shard_map.68 = (bf16[128,128]{1,0:T(8,128)(2,1)S(1)}, bf16[512,128]{1,0:T(8,128)(2,1)S(1)}) custom-call(s32[2]{0:T(128)} %bitcast.5, s32[1,1]{1,0:T(1,128)S(6)} %copy.7.count_in, bf16[128,128]{1,0:T(8,128)(2,1)} %user_in.1, bf16[2,256,128]{2,1,0:T(8,128)(2,1)} %bitcast.4, bf16[4,128,512]{2,1,0:T(8,128)(2,1)} %bitcast.3), custom_call_target="tpu_custom_call" | custom-call | tf_op jit(solution)/shard_map/pallas_call | solution.py:462
  19.0 0.7 %shard_map.69 = (bf16[128,128]{1,0:T(8,128)(2,1)}, bf16[512,128]{1,0:T(8,128)(2,1)}) custom-call(bf16[128,128]{1,0:T(8,128)(2,1)S(1)} %get-tuple-element.4.users, bf16[512,128]{1,0:T(8,128)(2,1)S(1)} %get-tuple-element.5.items), custom_call_target="tpu_custom_call" | custom-call | tf_op jit(solution)/shard_map/pallas_call | solution.py:511

commit v5 on v4

--- a/solution.py
+++ b/solution.py
@@ -156,6 +156,7 @@
     half, each = rows_i // 2, steps // groups
     chunk = half // steps
     pieces = size // rows_u // 2
+    turns = [(others[0] + step) % pieces for step in range(pieces)]
     sizes = []
 
     def user_slot(at):
@@ -300,16 +301,16 @@
         item_sel = jnp.concatenate([i_got[0, sel_x], i_got[1, sel_y]], axis=0)
         item_sel = jnp.where(live, item_sel, 0.0).astype(item_sel.dtype)
 
-        def multiply(owner):
-            rows = jnp.concatenate([tile_v[2 * h + owner] for h in range(pieces)], axis=0)
+        def multiply(some):
+            rows = jnp.concatenate([tile_v[b] for b in some], axis=0)
             product = jnp.dot(rows, item_sel, preferred_element_type=jnp.float32)
-            for h in range(pieces):
-                part_u[2 * h + owner] = product[h * rows_u : (h + 1) * rows_u]
-
-        multiply(core)
-        for h in range(pieces):
-            copy(part_u.at[2 * h + core], from_p.at[h], sent.at[0], rp_r.at[0], p_dev).start()
-        multiply(1 - core)
+            for at, b in enumerate(some):
+                part_u[b] = product[at * rows_u : (at + 1) * rows_u]
+
+        multiply([2 * h + core for h in turns])
+        for h in turns:
+            copy(part_u.at[2 * h + core], from_p.at[h], sent.at[0], rp_r.at[h], p_dev).start()
+        multiply([2 * h + 1 - core for h in range(pieces)])
 
     def items_product():
         arrived(u_all.at[pl.ds(0, u_all.shape[0] // 2)], up_r.at[0])
@@ -342,10 +343,13 @@
     for ref in (from_p, peak_1, peak_1, peak_1, send_1, send_1):
         sizes.append(math.prod(ref.shape) * ref.dtype.itemsize)
 
-    def users_out():
-        arrived(from_p, rp_r.at[0])
-        to = list(zip(others, z_devs))
-        for at, device in to[:1] + to[n_z // 2 :] + [(z, p_dev)] + to[1 : n_z // 2]:
+    targets = list(zip(others, z_devs))
+    targets = targets[:1] + targets[n_z // 2 :] + [(z, p_dev)] + targets[1 : n_z // 2]
+
+    def users_out(ready, some):
+        for h in ready:
+            arrived(from_p.at[h], rp_r.at[h])
+        for at, device in some:
             tile, h = at // pieces, at % pieces
             send_z[at], peak_z[at] = encode(
                 jnp.where(my_tu == tile, part_u[2 * h + 1 - core], 0.0)
@@ -353,6 +357,12 @@
             )
             copy(peak_z.at[at], from_zp.at[z], sent.at[0], rz_r.at[0], device).start()
             copy(send_z.at[at], from_z.at[z], sent.at[0], rz_r.at[0], device).start()
+
+    def users_first():
+        users_out(turns[:1], targets[:1])
+
+    def users_rest():
+        users_out(turns[1:], targets[1:])
 
     def items_out():
         landed(rq_r.at[0], pair_1, pair_1p)
@@ -389,22 +399,21 @@
     for ref in (peak_z, send_z, mask_1p, peak_2, send_2, from_1):
         sizes.append(math.prod(ref.shape) * ref.dtype.itemsize)
 
+    def run(*stages):
+        for stage in stages:
+            stage()
+
     @pl.when(high == 0)
     def _():
-        pass_across()
-        items_product()
-        users_product()
-        users_out()
-        items_out()
-
-    @pl.when(high == 1)
-    def _():
-        pass_across()
-        users_product()
-        items_product()
-        users_out()
-        items_out()
-
+        run(pass_across, items_product, users_product, users_first, users_rest, items_out)
+
+    @pl.when(jnp.logical_and(high == 1, z < n_z - 1))
+    def _():
+        run(pass_across, users_product, items_product, users_first, users_rest, items_out)
+
+    @pl.when(z == n_z - 1)
+    def _():
+        run(pass_across, users_product, users_first, items_product, users_rest, items_out)
 
     for step in range(steps):
         g = step // each
@@ -499,7 +508,7 @@
         ]
         + [dma((n,)) for n in (4, 1, 1)]
         + [pltpu.SemaphoreType.REGULAR]
-        + [dma((n,)) for n in (n_z, 1, 1, STEPS, 1, 1, 1, STEPS, 1, STEPS)],
+        + [dma((n,)) for n in (n_z, 1, 1, STEPS, 1, blocks // 2, 1, STEPS, 1, STEPS)],
         compiler_params=pltpu.CompilerParams(collective_id=0, has_side_effects=True),
     )(
         tile_coords.reshape(2),

time: 19.8 us -> 19.7 us (level)
  no operation moved by 1% of the time
where the time goes in v5:
time: 19.7 us; the launch traced here: 19.6 us
  Pallas kernels  18.3 us (93%)
  between operations  1.29 us (7%)
    pallas_call x1, Pallas kernels, planned(): pl.pallas_call(functools.partial(kernel, n_z), out_shape=(pltpu.VMEM((row...  17.6 us
    pallas_call x1, Pallas kernels, planned(): pl.pallas_call(put, out_shape=[jax.ShapeDtypeStruct(out.shape, out.dtype)...  0.69 us

profile of v5, /device:TPU:1, one launch (start us, length us, event | category | flops | bytes accessed | tf_op | source)
XLA Modules:
  0.0 19.6 jit_solution(13786299660972657060)
XLA Ops:
  1.3 17.6 %shard_map.68 = (bf16[128,128]{1,0:T(8,128)(2,1)S(1)}, bf16[512,128]{1,0:T(8,128)(2,1)S(1)}) custom-call(s32[2]{0:T(128)} %bitcast.5, s32[1,1]{1,0:T(1,128)S(6)} %copy.7.count_in, bf16[128,128]{1,0:T(8,128)(2,1)} %user_in.1, bf16[2,256,128]{2,1,0:T(8,128)(2,1)} %bitcast.4, bf16[4,128,512]{2,1,0:T(8,128)(2,1)} %bitcast.3), custom_call_target="tpu_custom_call" | custom-call | tf_op jit(solution)/shard_map/pallas_call | solution.py:471
  18.9 0.7 %shard_map.69 = (bf16[128,128]{1,0:T(8,128)(2,1)}, bf16[512,128]{1,0:T(8,128)(2,1)}) custom-call(bf16[128,128]{1,0:T(8,128)(2,1)S(1)} %get-tuple-element.4.users, bf16[512,128]{1,0:T(8,128)(2,1)S(1)} %get-tuple-element.5.items), custom_call_target="tpu_custom_call" | custom-call | tf_op jit(solution)/shard_map/pallas_call | solution.py:520

commit v6 on v5

--- a/solution.py
+++ b/solution.py
@@ -10,7 +10,7 @@
 
 MESH = pl.DeviceIdType.MESH
 LEVELS = 32760.0
-STEPS = 4
+STEPS = 8
 GROUPS = 2
 TINY = 1e-30
 
@@ -59,7 +59,8 @@
 def encode(values):
     rows, width = values.shape
     groups = values.reshape(rows // 8, 8, width)
-    peak = jnp.maximum(jnp.max(jnp.abs(groups), axis=0), TINY)
+    peak = jnp.max(jnp.max(jnp.abs(groups), axis=0), axis=0, keepdims=True)
+    peak = jnp.maximum(peak, TINY)
     return encode_by(values, peak), peak
 
 
@@ -465,7 +466,8 @@
     vmem = pl.BlockSpec(memory_space=pltpu.VMEM)
     anywhere = pl.BlockSpec(memory_space=pl.ANY)
     cut = (2, STEPS, rows_i // (2 * STEPS), width)
-    peak = (8, width)
+    peak = (1, width)
+    tag = (8, width)
     i16 = jnp.int16
     vm = pltpu.VMEM
     outs = pl.pallas_call(
@@ -481,8 +483,8 @@
             vm((2, rows_i // 2, width), bf16),
             vm((blocks, rows_u, size), bf16),
             vm((size, size), bf16),
-            vm((2,) + peak, jnp.int32),
-            vm((3, 2) + peak, jnp.int32),
+            vm((2,) + tag, jnp.int32),
+            vm((3, 2) + tag, jnp.int32),
             vm((blocks, rows_u, width), f32),
             vm((blocks // 2, rows_u, width), f32),
             vm((n_z, rows_u, width), i16),

time: 19.7 us -> 19.2 us (0.975)
  Pallas kernels: 18.3 us -> 17.6 us
    pallas_call x1, Pallas kernels: 17.6 us -> 16.9 us  [planned(): pl.pallas_call(functools.partial(kernel, n_z), out_shape=(pltpu.VMEM((row...]
where the time goes in v6:
time: 19.2 us; the launch traced here: 18.9 us
  Pallas kernels  17.6 us (92%)
  between operations  1.29 us (7%)
    pallas_call x1, Pallas kernels, planned(): pl.pallas_call(functools.partial(kernel, n_z), out_shape=(pltpu.VMEM((row...  16.9 us
    pallas_call x1, Pallas kernels, planned(): pl.pallas_call(put, out_shape=[jax.ShapeDtypeStruct(out.shape, out.dtype)...  0.69 us

profile of v6, /device:TPU:1, one launch (start us, length us, event | category | flops | bytes accessed | tf_op | source)
XLA Modules:
  0.0 18.9 jit_solution(10717992290897689799)
XLA Ops:
  1.3 16.9 %shard_map.68 = (bf16[128,128]{1,0:T(8,128)(2,1)S(1)}, bf16[512,128]{1,0:T(8,128)(2,1)S(1)}) custom-call(s32[2]{0:T(128)} %bitcast.5, s32[1,1]{1,0:T(1,128)S(6)} %copy.7.count_in, bf16[128,128]{1,0:T(8,128)(2,1)} %user_in.1, bf16[2,256,128]{2,1,0:T(8,128)(2,1)} %bitcast.4, bf16[4,128,512]{2,1,0:T(8,128)(2,1)} %bitcast.3), custom_call_target="tpu_custom_call" | custom-call | tf_op jit(solution)/shard_map/pallas_call | solution.py:473
  18.2 0.7 %shard_map.69 = (bf16[128,128]{1,0:T(8,128)(2,1)}, bf16[512,128]{1,0:T(8,128)(2,1)}) custom-call(bf16[128,128]{1,0:T(8,128)(2,1)S(1)} %get-tuple-element.4.users, bf16[512,128]{1,0:T(8,128)(2,1)S(1)} %get-tuple-element.5.items), custom_call_target="tpu_custom_call" | custom-call | tf_op jit(solution)/shard_map/pallas_call | solution.py:522

commit v7 on v6

--- a/solution.py
+++ b/solution.py
@@ -190,14 +190,13 @@
         arrived(gauge.at[pl.ds(0, total // (4 * width))], recv)
 
     barrier = pltpu.get_barrier_semaphore()
-    across, mates = z_devs[: n_z // 2], z_devs[n_z // 2 :]
-    peers = [x_dev, y_dev, p_dev] + mates
+    peers = [x_dev, y_dev, p_dev]
     for peer in peers:
         pl.semaphore_signal(barrier, inc=1, device_id=peer, device_id_type=MESH)
-
-    @pl.when(high == 0)
-    def _():
-        for peer in across:
+    for at, peer in zip(others, z_devs):
+
+        @pl.when(at > z)
+        def _():
             pl.semaphore_signal(barrier, inc=1, device_id=peer, device_id_type=MESH)
 
     loads = [
@@ -215,20 +214,27 @@
     meta[1] = jnp.full(meta.shape[1:], ti, jnp.int32)
     my_tu, my_ti = meta[0][0:1, :], meta[1][0:1, :]
     live = jnp.full((1, width), count_in[0, 0], jnp.int32) > 0
-    pl.semaphore_wait(barrier, len(peers) + high * len(across))
+    pl.semaphore_wait(barrier, len(peers) + z)
 
     loads[0].wait()
     own = user_slot(col)
 
-    @pl.when(high == 1)
+    bottom, top = (row, 1 - core), (row, 2 * (n_z - 1) + 1 - core)
+
+    def send_own(device, sem):
+        copy(own, own, sem.at[0], uz_r.at[z], device).start()
+
+    @pl.when(z > 0)
     def _():
-        for peer in across:
+        send_own(bottom, first_s)
+
+    for at, peer in zip(others, z_devs):
+
+        @pl.when(at < z)
+        def _():
             pl.semaphore_signal(late, inc=1, device_id=peer, device_id_type=MESH)
-        copy(own, own, first_s.at[0], uz_r.at[z], across[0]).start()
-
-    sizes.extend([rows_u * width * 2] * (len(across) - 1))
-    for device in mates:
-        send(own, own, uz_r.at[z], device)
+
+    sizes.extend([rows_u * width * 2] * (n_z - 2))
     for at, device in enumerate((x_dev, y_dev, p_dev)):
         send(meta, metas.at[at], io_r.at[0], device)
     loads[1].wait()
@@ -246,11 +252,15 @@
 
     loads[2].wait()
     tile_t[...] = tile_v[...].reshape(size, size).T
-    @pl.when(high == 1)
+    @pl.when(z > 0)
     def _():
-        copy(own, own, first_s.at[0], uz_r.at[z], across[0]).wait_send()
-        for device in across[1:]:
-            copy(own, own, sent.at[0], uz_r.at[z], device).start()
+        copy(own, own, first_s.at[0], uz_r.at[z], bottom).wait_send()
+
+    for at, device in zip(others, z_devs):
+
+        @pl.when(jnp.logical_and(at > 0, at < z))
+        def _():
+            send_own(device, sent)
 
     landed(io_r.at[0], metas, r_own)
     x_ti, y_ti, p_ti = (metas[at, 1][0:1, :] for at in range(3))
@@ -277,21 +287,29 @@
     items = [(pass_items, step) for step in range(steps)]
     sizes.extend([rows_u * width * 2] * len(users) + [chunk * width * 2] * (4 * steps))
 
-    for step, at in users[: len(mates)]:
+    def send_up():
+        @pl.when(z < n_z - 1)
+        def _():
+            pl.semaphore_wait(late, n_z - 1 - z)
+
+        for at, device in list(zip(others, z_devs))[::-1]:
+
+            @pl.when(jnp.logical_and(at > z, jnp.logical_or(z > 0, at < n_z - 1)))
+            def _():
+                send_own(device, sent)
+
+        @pl.when(z == 0)
+        def _():
+            send_own(top, first_s)
+
+    for step, at in items[: steps // 2]:
         step(at)
-
-    @pl.when(high == 0)
-    def _():
-        pl.semaphore_wait(late, len(across))
-        for device in across[:0:-1]:
-            copy(own, own, sent.at[0], uz_r.at[z], device).start()
-        copy(own, own, first_s.at[0], uz_r.at[z], across[0]).start()
-
-    for step, at in items:
+    send_up()
+    for step, at in items[steps // 2 :]:
         step(at)
 
     def pass_across():
-        for step, at in users[len(mates) :]:
+        for step, at in users:
             step(at)
 
 
@@ -414,7 +432,7 @@
 
     @pl.when(z == n_z - 1)
     def _():
-        run(pass_across, users_product, users_first, items_product, users_rest, items_out)
+        run(users_product, pass_across, users_first, items_product, users_rest, items_out)
 
     for step in range(steps):
         g = step // each
@@ -438,9 +456,9 @@
         total = total + decode(from_z[at], from_zp[at])
     out_u[...] = total.astype(out_u.dtype)
 
-    @pl.when(high == 0)
+    @pl.when(z == 0)
     def _():
-        copy(own, own, first_s.at[0], uz_r.at[z], across[0]).wait_send()
+        copy(own, own, first_s.at[0], uz_r.at[z], top).wait_send()
 
     like = gauge.at[pl.ds(0, sum(sizes) // (4 * width))]
     copy(like, like, sent.at[0], sent.at[0], x_dev).wait_send()

time: 19.2 us -> 19.1 us (level)
  the two profiles are of different devices: /device:TPU:1 before, /device:TPU:0 now
where the time goes in v7:
time: 19.1 us; the launch traced here: 18.9 us
  Pallas kernels  17.6 us (92%)
  between operations  1.29 us (7%)
    pallas_call x1, Pallas kernels, planned(): pl.pallas_call(functools.partial(kernel, n_z), out_shape=(pltpu.VMEM((row...  16.9 us
    pallas_call x1, Pallas kernels, planned(): pl.pallas_call(put, out_shape=[jax.ShapeDtypeStruct(out.shape, out.dtype)...  0.69 us

profile of v7, /device:TPU:0, one launch (start us, length us, event | category | flops | bytes accessed | tf_op | source)
XLA Modules:
  0.0 18.9 jit_solution(3812935957530390005)
XLA Ops:
  1.3 16.9 %shard_map.68 = (bf16[128,128]{1,0:T(8,128)(2,1)S(1)}, bf16[512,128]{1,0:T(8,128)(2,1)S(1)}) custom-call(s32[2]{0:T(128)} %bitcast.5, s32[1,1]{1,0:T(1,128)S(6)} %copy.7.count_in, bf16[128,128]{1,0:T(8,128)(2,1)} %user_in.1, bf16[2,256,128]{2,1,0:T(8,128)(2,1)} %bitcast.4, bf16[4,128,512]{2,1,0:T(8,128)(2,1)} %bitcast.3), custom_call_target="tpu_custom_call" | custom-call | tf_op jit(solution)/shard_map/pallas_call | solution.py:491
  18.2 0.7 %shard_map.69 = (bf16[128,128]{1,0:T(8,128)(2,1)}, bf16[512,128]{1,0:T(8,128)(2,1)}) custom-call(bf16[128,128]{1,0:T(8,128)(2,1)S(1)} %get-tuple-element.4.users, bf16[512,128]{1,0:T(8,128)(2,1)S(1)} %get-tuple-element.5.items), custom_call_target="tpu_custom_call" | custom-call | tf_op jit(solution)/shard_map/pallas_call | solution.py:540

commit v8 on v7

--- a/solution.py
+++ b/solution.py
@@ -428,7 +428,7 @@
 
     @pl.when(jnp.logical_and(high == 1, z < n_z - 1))
     def _():
-        run(pass_across, users_product, items_product, users_first, users_rest, items_out)
+        run(users_product, pass_across, items_product, users_first, users_rest, items_out)
 
     @pl.when(z == n_z - 1)
     def _():

time: 19.1 us -> 19 us (level)
  the two profiles are of different devices: /device:TPU:0 before, /device:TPU:1 now
where the time goes in v8:
time: 19 us; the launch traced here: 18.6 us
  Pallas kernels  17.3 us (91%)
  between operations  1.29 us (7%)
    pallas_call x1, Pallas kernels, planned(): pl.pallas_call(functools.partial(kernel, n_z), out_shape=(pltpu.VMEM((row...  16.7 us
    pallas_call x1, Pallas kernels, planned(): pl.pallas_call(put, out_shape=[jax.ShapeDtypeStruct(out.shape, out.dtype)...  0.69 us

profile of v8, /device:TPU:1, one launch (start us, length us, event | category | flops | bytes accessed | tf_op | source)
XLA Modules:
  0.0 18.6 jit_solution(17379351451208831702)
XLA Ops:
  1.3 16.7 %shard_map.68 = (bf16[128,128]{1,0:T(8,128)(2,1)S(1)}, bf16[512,128]{1,0:T(8,128)(2,1)S(1)}) custom-call(s32[2]{0:T(128)} %bitcast.5, s32[1,1]{1,0:T(1,128)S(6)} %copy.7.count_in, bf16[128,128]{1,0:T(8,128)(2,1)} %user_in.1, bf16[2,256,128]{2,1,0:T(8,128)(2,1)} %bitcast.4, bf16[4,128,512]{2,1,0:T(8,128)(2,1)} %bitcast.3), custom_call_target="tpu_custom_call" | custom-call | tf_op jit(solution)/shard_map/pallas_call | solution.py:491
  17.9 0.7 %shard_map.69 = (bf16[128,128]{1,0:T(8,128)(2,1)}, bf16[512,128]{1,0:T(8,128)(2,1)}) custom-call(bf16[128,128]{1,0:T(8,128)(2,1)S(1)} %get-tuple-element.4.users, bf16[512,128]{1,0:T(8,128)(2,1)S(1)} %get-tuple-element.5.items), custom_call_target="tpu_custom_call" | custom-call | tf_op jit(solution)/shard_map/pallas_call | solution.py:540
